TPU v7x, 32 devices: a whole 2x2x4 slice. The times are simulated.
32 devices in a mesh: tile: 8 (over z, x), mem: 4 (over y, core).
Axes of the slice: x: 2, y: 2, z: 4, core: 2. Of those that a mesh axis runs over, the one named last changes fastest.
Arguments:
- ensemble: bfloat16 [64, 128, 1024], P('mem', 'tile'), may hold values from -8 to 8
- obs_members: bfloat16 [4096, 64, 128], P(('tile', 'mem')), may hold values from -6 to 6
- obs_values: float32 [4096, 128], P(('tile', 'mem')), may hold values from -9 to 9
- obs_weight: float32 [4096, 128], P(('tile', 'mem')), may hold values from 0.05 to 1
- obs_count: int32 [4096], P(('tile', 'mem')), may hold values from 1 to 128
- obs_tile: int32 [4096], P(('tile', 'mem')), may hold values from 0 to 7, as said below
- obs_block: int32 [4096], P(('tile', 'mem')), may hold values from 0 to 15
- obs_turn: int32 [4096], P(('tile', 'mem')), may hold values from 0 to 3
Outputs:
- analysis_pert: bfloat16 [64, 128, 1024], P('mem', 'tile')
- analysis_mean: bfloat16 [128, 1024], P(('tile', 'mem'))
Inputs may be any that keep to these rules, and one draw needn't show every extreme that they name: `obs_tile`: within each aligned group of 128 consecutive blocks (the blocks of one device), no tile is named more than 32 times, and one tile is named exactly 32 times by every group.
All inputs are finite; a program needn't handle non-finite values.
Results may differ from a plain program's by a relative error of at most 0.0036.
Values may be sent and summed in bfloat16 or wider, within the bound.
No kernel may reach another device: no remote copies, remote signals or barrier semaphores. Data moves between devices by JAX's collectives and lax.ppermute only.
A program may use at most 64 MiB of HBM per device.

v0:
```python
import jax
import jax.numpy as jnp
import numpy as np
from jax import lax
from jax.sharding import PartitionSpec as P

MEMBERS = 64
BPS = 4
OBD = 128
NS_STEPS = 6
ABLK = 16


def product(left, right):
    return jnp.matmul(left, right, precision=lax.Precision.HIGHEST)


def target_block(obs_block, obs_turn):
    block_row = obs_block // BPS
    block_col = obs_block % BPS
    last = BPS - 1
    new_row = jnp.where(
        obs_turn == 0,
        block_row,
        jnp.where(
            obs_turn == 1, block_col, jnp.where(obs_turn == 2, last - block_row, last - block_col)
        ),
    )
    new_col = jnp.where(
        obs_turn == 0,
        block_col,
        jnp.where(
            obs_turn == 1, last - block_row, jnp.where(obs_turn == 2, last - block_col, block_row)
        ),
    )
    return new_row * BPS + new_col


def scaled_obs(obs_members, obs_values, obs_weight, obs_count):
    obs_mean = jnp.sum(obs_members, axis=1, dtype=jnp.float32) / MEMBERS
    usable = lax.broadcasted_iota(jnp.int32, obs_weight.shape, 1) < obs_count[:, None]
    weight_root = jnp.sqrt(jnp.where(usable, obs_weight, jnp.zeros_like(obs_weight)))
    scaled_pert = (
        (obs_members.astype(jnp.float32) - obs_mean[:, None, :]) * weight_root[:, None, :]
    ).astype(jnp.bfloat16)
    scaled_innov = ((obs_values - obs_mean) * weight_root).astype(jnp.bfloat16)
    return (scaled_pert, scaled_innov)


def transforms(gram, projection):
    identity = jnp.eye(MEMBERS, dtype=jnp.float32)
    system = (MEMBERS - 1.0) * identity + gram
    frob = jnp.sqrt(jnp.sum(system * system, axis=(1, 2)))[:, None, None]
    square_root = system / frob
    inverse = jnp.broadcast_to(identity, system.shape)
    for sweep in range(NS_STEPS):
        middle = 1.5 * identity - 0.5 * product(inverse, square_root)
        square_root = product(square_root, middle)
        inverse = product(middle, inverse)
    inverse_root = inverse / jnp.sqrt(frob)
    covariance = product(inverse_root, inverse_root)
    mean_weights = jnp.einsum(
        "bjk,bk->bj", covariance, projection, precision=lax.Precision.HIGHEST
    ).astype(jnp.bfloat16)
    spread = (jnp.sqrt(MEMBERS - 1.0) * inverse_root).astype(jnp.bfloat16)
    return (spread, mean_weights)


def triangle_tables(members):
    upper_row, upper_col = np.triu_indices(members)
    packed_flat = (upper_row * members + upper_col).astype(np.int32)
    lookup = np.zeros((members, members), np.int32)
    lookup[upper_row, upper_col] = np.arange(upper_row.shape[0], dtype=np.int32)
    lookup[upper_col, upper_row] = np.arange(upper_row.shape[0], dtype=np.int32)
    return (packed_flat, lookup.reshape(-1))


def body(ensemble, obs_members, obs_values, obs_weight, obs_count, obs_tile, obs_block, obs_turn):
    tile_count = lax.axis_size("tile")
    groups = lax.axis_size("mem")
    group_index = lax.axis_index("mem")
    capacity = max(2, 2 * OBD // tile_count)
    slot_count = tile_count * capacity
    own_blocks = ABLK // groups
    member_share = ensemble.shape[0]
    scaled_pert, scaled_innov = scaled_obs(obs_members, obs_values, obs_weight, obs_count)
    target = target_block(obs_block, obs_turn)
    later = lax.broadcasted_iota(jnp.int32, (OBD, OBD), 0) > lax.broadcasted_iota(
        jnp.int32, (OBD, OBD), 1
    )
    same_tile = obs_tile[:, None] == obs_tile[None, :]
    arrival = jnp.sum((later & same_tile).astype(jnp.int32), axis=1)
    position = obs_tile * capacity + arrival
    packed_flat, lookup = triangle_tables(MEMBERS)
    entries = packed_flat.shape[0]
    padded_width = (entries + 127) // 128 * 128
    own_gram = jnp.einsum(
        "nkr,nlr->nkl", scaled_pert, scaled_pert, preferred_element_type=jnp.float32
    )
    own_proj = jnp.einsum(
        "nkr,nr->nk", scaled_pert, scaled_innov, preferred_element_type=jnp.float32
    )
    packed = jnp.take(own_gram.reshape(OBD, MEMBERS * MEMBERS), jnp.asarray(packed_flat), axis=1)
    packed = jnp.pad(packed, ((0, 0), (0, padded_width - entries)))
    send_packed = jnp.zeros((slot_count, padded_width), jnp.float32).at[position].set(packed)
    send_proj = jnp.zeros((slot_count, MEMBERS), jnp.float32).at[position].set(own_proj)
    send_target = (
        jnp.zeros((slot_count, 1), jnp.float32)
        .at[position]
        .set(target.astype(jnp.float32)[:, None])
    )
    got_packed, slot_proj, got_target = (
        lax.all_to_all(send_packed, "tile", split_axis=0, concat_axis=0, tiled=True),
        lax.all_to_all(send_proj, "tile", split_axis=0, concat_axis=0, tiled=True),
        lax.all_to_all(send_target, "tile", split_axis=0, concat_axis=0, tiled=True),
    )
    slot_gram = jnp.take(got_packed, jnp.asarray(lookup), axis=1).reshape(
        slot_count, MEMBERS, MEMBERS
    )
    block_ids = jnp.arange(ABLK, dtype=jnp.float32)[None, :]
    belongs = (got_target == block_ids).astype(jnp.float32)
    gram = jnp.einsum("sb,skl->bkl", belongs, slot_gram, precision=lax.Precision.HIGHEST)
    projection = jnp.einsum("sb,sk->bk", belongs, slot_proj, precision=lax.Precision.HIGHEST)
    gram, projection = lax.psum((gram, projection), "mem")
    spread, mean_weights = transforms(gram, projection)
    member_total = lax.psum(jnp.sum(ensemble, axis=0, dtype=jnp.float32), "mem")
    background_mean = member_total / MEMBERS
    perturbation = (ensemble.astype(jnp.float32) - background_mean[None]).astype(jnp.bfloat16)
    own_spread = lax.dynamic_slice_in_dim(spread, group_index * member_share, member_share, 2)
    own_weights = lax.dynamic_slice_in_dim(mean_weights, group_index * own_blocks, own_blocks, 0)
    shard_rows = lax.all_gather(perturbation, "mem", axis=0, tiled=True)
    pert_total = jnp.einsum(
        "jbx,bjk->kbx", shard_rows, own_spread, preferred_element_type=jnp.float32
    )
    block_rows = lax.dynamic_slice_in_dim(shard_rows, group_index * own_blocks, own_blocks, 1)
    mean_total = jnp.einsum(
        "jbx,bj->bx", block_rows, own_weights, preferred_element_type=jnp.float32
    )
    pert_total, mean_total = (pert_total, mean_total)
    own_mean = lax.dynamic_slice_in_dim(background_mean, group_index * own_blocks, own_blocks, 0)
    return (pert_total.astype(jnp.bfloat16), (own_mean + mean_total).astype(jnp.bfloat16))


def solution(mesh):
    placed = (
        P("mem", "tile", None),
        P(("tile", "mem"), None, None),
        P(("tile", "mem"), None),
        P(("tile", "mem"), None),
        P(("tile", "mem")),
        P(("tile", "mem")),
        P(("tile", "mem")),
        P(("tile", "mem")),
    )
    return jax.shard_map(
        body,
        mesh=mesh,
        in_specs=placed,
        out_specs=(P("mem", "tile", None), P(("tile", "mem"), None)),
        check_vma=False,
    )
```

profile of v0, /device:TPU:0, one launch (start us, length us, event | category | flops | bytes accessed | tf_op | source)
XLA Modules:
  0.0 200.4 jit_solution(14732286319261956822)
XLA Ops:
  10.6 7.3 %all-to-all-start = ((f32[8,32,1]{1,2,0:T(1,128)}), f32[8,32,1]{1,2,0:T(1,128)S(1)}, u32[]{:S(2)}, u32[]{:S(2)}) async-start(f32[8,32,1]{1,2,0:T(1,128)} %bitcast), calls=%async_computation | async-start | bytes 8192 | tf_op jit(solution)/shard_map/all_to_all | solution.py:115
  17.8 2.2 %convert_reduce_fusion = f32[128,128]{1,0:T(8,128)S(1)} fusion(bf16[128,64,128]{2,1,0:T(8,128)(2,1)} %param.11), kind=kLoop, calls=%fused_computation.6 | loop fusion | flops 2080768 | bytes 2162688 | tf_op jit(solution)/shard_map/reduce_sum | solution.py:40
  21.1 1.2 fusion.2
  24.3 5.7 %all-to-all-start.2 = ((f32[8,1,2048]{2,1,0:T(1,128)}), f32[8,1,2048]{2,1,0:T(1,128)S(1)}, u32[]{:S(2)}, u32[]{:S(2)}) async-start(f32[8,1,2048]{2,1,0:T(1,128)} %reshape.129), calls=%async_computation.2 | async-start | bytes 131072 | tf_op jit(solution)/shard_map/all_to_all | solution.py:114
  29.9 3.2 %fusion.4 = f32[128,64,64]{2,1,0:T(8,128)} fusion(bf16[128,64,128]{2,1,0:T(8,128)(2,1)S(1)} %copy-done.1, f32[128,128]{1,0:T(8,128)S(1)} %get-tuple-element.13, f32[128,128]{1,0:T(8,128)S(1)} %get-tuple-element.14), kind=kOutput, calls=%fused_computation.10 | convolution fusion | flops 138412032 | bytes 4325376 | tf_op jit(solution)/shard_map/nkr,nlr->nkl/dot_general | solution.py:97
  33.1 3.8 %copy.38 = f32[128,64,64]{0,2,1:T(8,128)S(1)} copy(f32[128,64,64]{2,1,0:T(8,128)} %fusion.4) | data formatting | bytes 4194304 | tf_op jit(solution)/shard_map/nkr,nlr->nkl/dot_general | solution.py:97
  36.9 3.9 %gather_fusion = f32[2080,128]{1,0:T(8,128)S(1)} fusion(f32[128,4096]{0,1:T(8,128)S(1)} %bitcast.68, s32[3072]{0:T(1024)S(1)} %pad_clamp_fusion), kind=kCustom, calls=%fused_computation | custom fusion | bytes 2138240 | tf_op jit(solution)/shard_map/jit(_take)/gather | solution.py:103
  41.3 2.8 %scatter_custom_fusion.1 = f32[256,2176]{1,0:T(8,128)} fusion(s32[128]{0:T(128)S(1)} %get-tuple-element.17, f32[128,2080]{1,0:T(8,128)S(1)} %copy.57, f32[]{:T(128)} %constant.48.clone.1), kind=kCustom, calls=%fused_computation.28 | custom fusion | bytes 3343360 | tf_op jit(solution)/shard_map/scatter | solution.py:105
  44.1 6.1 %all-to-all-start.1 = ((f32[8,32,2176]{2,1,0:T(8,128)}), f32[8,32,2176]{2,1,0:T(8,128)S(1)}, u32[]{:S(2)}, u32[]{:S(2)}) async-start(f32[8,32,2176]{2,1,0:T(8,128)} %bitcast.4), calls=%async_computation.1 | async-start | bytes 4456448 | tf_op jit(solution)/shard_map/all_to_all | solution.py:113
  54.0 46.1 %all-to-all-done.1 = f32[8,32,2176]{2,1,0:T(8,128)S(1)} async-done(((f32[8,32,2176]{2,1,0:T(8,128)}), f32[8,32,2176]{2,1,0:T(8,128)S(1)}, u32[]{:S(2)}, u32[]{:S(2)}) %all-to-all-start.1) | async-done | bytes 2228256 | tf_op jit(solution)/shard_map/all_to_all | solution.py:113
  100.1 1.4 copy-done
  101.5 2.0 copy.40
  103.5 16.1 %gather_fusion.1 = f32[4096,256]{1,0:T(8,128)} fusion(f32[256,2176]{0,1:T(8,128)S(1)} %copy.40, s32[4096]{0:T(1024)S(1)} %broadcast_clamp_fusion), kind=kCustom, calls=%fused_computation.1 | custom fusion | bytes 8404992 | tf_op jit(solution)/shard_map/jit(_take)/gather | solution.py:117
  119.6 5.5 %fusion.39 = f32[16,64,64]{2,0,1:T(8,128)} fusion(f32[256,64,64]{0,2,1:T(8,128)} %bitcast.69, f32[256]{0:T(256)S(1)} %eq.75), kind=kOutput, calls=%fused_computation.66 | convolution fusion | flops 201330688 | bytes 4457472 | tf_op jit(solution)/shard_map/sb,skl->bkl/dot_general | solution.py:122
  125.4 5.9 %psum.23 = f32[16,64]{1,0:T(8,128)S(1)} all-reduce(f32[16,64]{1,0:T(8,128)S(1)} %fusion.37), channel_id=1, replica_groups=mesh['tile'=8,'mem'=4] {'mem'}, use_global_device_ids=true, to_apply=%region_9.10 | all-reduce | flops 1024 | bytes 8192 | tf_op jit(solution)/shard_map/psum | solution.py:124
  131.3 26.9 %all-reduce.4.cloned.1.call-done = (f32[16,1024]{1,0:T(8,128)}, f32[16,64,64]{2,0,1:T(8,128)}) async-done(((f32[16,1024]{1,0:T(8,128)}, f32[16,64,64]{2,0,1:T(8,128)}), (f32[16,1024]{1,0:T(8,128)}, f32[16,64,64]{2,0,1:T(8,128)})) %all-reduce.4.cloned.1.call-update) | async-done | bytes 327696 | tf_op jit(solution)/shard_map/psum | solution.py:126
  158.2 1.2 multiply_reduce_fusion
  159.5 1.2 add_divide_fusion
  164.8 1.1 fusion.16
  172.4 1.2 convolution_divide_fusion
  175.6 13.0 %all-gather.2.cloned.1.call-done = bf16[64,16,1024]{2,0,1:T(8,128)(2,1)} async-done(((bf16[16,16,1024]{2,0,1:T(8,128)(2,1)}), bf16[64,16,1024]{2,0,1:T(8,128)(2,1)}) %all-gather.2.cloned.1.call-update) | async-done | bytes 2097168 | tf_op jit(solution)/shard_map/all_gather | solution.py:131
  188.6 1.2 fusion.17
  190.5 2.0 fusion.6
  192.4 1.1 copy.47
  (64 shorter events, 23.7 us)
Async XLA Ops:
  7.2 13.9 %copy-start.1 = (bf16[128,64,128]{2,1,0:T(8,128)(2,1)S(1)}, bf16[128,64,128]{2,1,0:T(8,128)(2,1)}, u32[]{:S(2)}) copy-start(bf16[128,64,128]{2,1,0:T(8,128)(2,1)} %param.11) | copy-start | bytes 6291460
  7.2 12.9 %copy-start.4 = (f32[128,128]{1,0:T(8,128)S(1)}, f32[128,128]{1,0:T(8,128)}, u32[]{:S(2)}) copy-start(f32[128,128]{1,0:T(8,128)} %param.12) | copy-start | bytes 196612
  7.2 12.9 %copy-start.7 = (s32[128]{0:T(128)S(1)}, s32[128]{0:T(128)}, u32[]{:S(2)}) copy-start(s32[128]{0:T(128)} %param.14) | copy-start | bytes 1540
  10.6 13.7 %all-to-all-start = ((f32[8,32,1]{1,2,0:T(1,128)}), f32[8,32,1]{1,2,0:T(1,128)S(1)}, u32[]{:S(2)}, u32[]{:S(2)}) async-start(f32[8,32,1]{1,2,0:T(1,128)} %bitcast), calls=%async_computation | async-start | bytes 8192 | tf_op jit(solution)/shard_map/all_to_all | solution.py:115
  24.3 19.8 %all-to-all-start.2 = ((f32[8,1,2048]{2,1,0:T(1,128)}), f32[8,1,2048]{2,1,0:T(1,128)S(1)}, u32[]{:S(2)}, u32[]{:S(2)}) async-start(f32[8,1,2048]{2,1,0:T(1,128)} %reshape.129), calls=%async_computation.2 | async-start | bytes 131072 | tf_op jit(solution)/shard_map/all_to_all | solution.py:114
  33.1 3.8 %copy-start.6 = (s32[2080]{0:T(1024)S(1)}, s32[2080]{0:T(1024)}, u32[]{:S(2)}) copy-start(s32[2080]{0:T(1024)} %constant.122) | copy-start | bytes 24964
  44.1 6.2 %copy-start.2 = (bf16[16,16,1024]{2,1,0:T(8,128)(2,1)S(1)}, bf16[16,16,1024]{2,1,0:T(8,128)(2,1)}, u32[]{:S(2)}) copy-start(bf16[16,16,1024]{2,1,0:T(8,128)(2,1)} %param.10) | copy-start | bytes 1572868
  44.1 7.3 %copy-start.5 = (s32[4096]{0:T(1024)S(1)}, s32[4096]{0:T(1024)}, u32[]{:S(2)}) copy-start(s32[4096]{0:T(1024)} %constant.123) | copy-start | bytes 49156
  44.1 56.1 %all-to-all-start.1 = ((f32[8,32,2176]{2,1,0:T(8,128)}), f32[8,32,2176]{2,1,0:T(8,128)S(1)}, u32[]{:S(2)}, u32[]{:S(2)}) async-start(f32[8,32,2176]{2,1,0:T(8,128)} %bitcast.4), calls=%async_computation.1 | async-start | bytes 4456448 | tf_op jit(solution)/shard_map/all_to_all | solution.py:113
  50.2 108.0 %all-reduce.4.cloned.1.call-start = ((), (), s32[]{:S(2)}) async-start(), calls=%async_computation.4 | async-start | bytes 1179648 | tf_op jit(solution)/shard_map/psum | solution.py:126
  100.1 1.4 copy-start
  125.2 63.5 %all-gather.2.cloned.1.call-start = ((), (), s32[]{:S(2)}) async-start(), calls=%async_computation.3 | async-start | bytes 2621440 | tf_op jit(solution)/shard_map/all_gather | solution.py:131
  162.8 2.0 copy-start.3
Sparse Core Ops, SparseCore 0:
  125.3 32.8 all-reduce.3
  166.0 22.5 all-gather.1
where the time goes:
time: 201 us; the launch traced here: 200 us
  waiting for transfers between devices  86.4 us (43%)
  local copies, waits for them, and re-layouts  36 us (18%)
  matrix products  26.9 us (13%)
  starting transfers between devices  19.2 us (10%)
  between operations  14.4 us (7%)
  other arithmetic  11.5 us (6%)
  blocking collectives  5.93 us (3%)
    all_to_all x1, waiting for transfers between devices, body(): lax.all_to_all(send_packed, 'tile', split_axis=0, concat_axis=0, tiled=True)  46.1 us
    psum x1, waiting for transfers between devices, body(): member_total = lax.psum(jnp.sum(ensemble, axis=0, dtype=jnp.float32), 'mem')  26.9 us
    gather x1, local copies, waits for them, and re-layouts, body(): jnp.take(got_packed, jnp.asarray(lookup), axis=1)  16.1 us
    all_gather x1, waiting for transfers between devices, body(): shard_rows = lax.all_gather(perturbation, 'mem', axis=0, tiled=True)  13 us
    dot_general x18, matrix products, product(): return jnp.matmul(left, right, precision=lax.Precision.HIGHEST)  12.7 us
    all_to_all x1, starting transfers between devices, body(): lax.all_to_all(send_target, 'tile', split_axis=0, concat_axis=0, tiled=True)  7.28 us
    all_to_all x1, starting transfers between devices, body(): lax.all_to_all(send_packed, 'tile', split_axis=0, concat_axis=0, tiled=True)  6.13 us
    psum x1, blocking collectives, body(): gram, projection = lax.psum((gram, projection), 'mem')  5.93 us
  transfers between devices with their start and end apart: 5, of which 4 were waited for; matrix products, arithmetic and copies ran while one was open for 17% of the time, Pallas kernels for 0%

commit v1 on v0

v1 whole, which is shorter than its diff:
```python
import functools

import jax
import jax.numpy as jnp
from jax import lax
from jax.experimental import pallas as pl
from jax.experimental.pallas import tpu as pltpu
from jax.sharding import Mesh, PartitionSpec as P

BPS = 4
ABLK = BPS * BPS
NS_STEPS = 6
CORES = 2
LANES = 128
F32 = jnp.float32
BF16 = jnp.bfloat16


def iota(shape, dim):
    return lax.broadcasted_iota(jnp.int32, shape, dim)


def packed_rows(own):
    return (16 * own + own + 7) // 8 * 8


def whole(shape=None):
    return pl.BlockSpec(memory_space=pltpu.VMEM)


def scalars():
    return pl.BlockSpec(memory_space=pltpu.SMEM)


def target_of(tile, block, turn):
    row, col = block // BPS, block % BPS
    last = BPS - 1
    new_row = jnp.where(
        turn == 0, row, jnp.where(turn == 1, col, jnp.where(turn == 2, last - row, last - col))
    )
    new_col = jnp.where(
        turn == 0, col, jnp.where(turn == 1, last - row, jnp.where(turn == 2, last - col, row))
    )
    return tile * ABLK + new_row * BPS + new_col


def gram_kernel(
    own, chunks, count, tile, block, turn, values, weight, members_hbm, send, keep, members, total, sems
):
    blocks, size, rows = members.shape
    per_chunk = blocks // chunks
    copies = [
        pltpu.make_async_copy(
            members_hbm.at[pl.ds(c * per_chunk, per_chunk)],
            members.at[pl.ds(c * per_chunk, per_chunk)],
            sems.at[c],
        )
        for c in range(chunks)
    ]
    for copy in copies:
        copy.start()

    def clear(t, _):
        total[t] = jnp.zeros(total.shape[1:], F32)
        return 0

    lax.fori_loop(0, total.shape[0], clear, 0, unroll=4)
    lane = iota((1, rows), 1)
    first = iota((16, rows), 0) == 0

    def add_block(n, _):
        perts = members[n].astype(F32)
        mean = jnp.sum(perts, axis=0, keepdims=True) / size
        root = jnp.sqrt(jnp.where(lane < count[n], weight[pl.ds(n, 1), :], 0.0))
        scaled = ((perts - mean) * root).astype(BF16)
        innov = (values[pl.ds(n, 1), :] - mean) * root
        tail = jnp.where(first, innov, 0.0).astype(BF16)
        left = jnp.concatenate([scaled, tail], axis=0)
        right = jnp.concatenate([scaled, scaled], axis=0)
        products = lax.dot_general(
            left, right, (((1,), (1,)), ((), ())), preferred_element_type=F32
        )
        t = target_of(tile[n], block[n], turn[n])
        total[t] = total[t] + products[: size + 8]
        return 0

    for c in range(chunks):
        copies[c].wait()
        lax.fori_loop(c * per_chunk, (c + 1) * per_chunk, add_block, 0, unroll=4)

    half = size // 2
    lane_half = iota((half, LANES), 1)
    col = lane_half % size
    row = iota((half, LANES), 0)
    from_top = (col >= half) | (col <= row)
    on_diag = col == row
    first_of_pair = iota((size + 8, LANES), 1) < size
    core = lax.axis_index("core")
    tail_row = iota((8, LANES), 0)

    def pack(d, side):
        base = d * (CORES * own) + side * own
        bodies = []
        tail = jnp.zeros((8, LANES), F32)
        for pair in range(own // 2):
            both = jnp.where(first_of_pair, total[base + 2 * pair], total[base + 2 * pair + 1])
            top = both[:half]
            bottom = pltpu.roll(both[half:size], LANES - half, 1)
            bodies.append(jnp.where(from_top, top, bottom))
            diag = jnp.sum(jnp.where(on_diag, bottom, 0.0), axis=0, keepdims=True)
            tail = jnp.where(tail_row == 2 * pair, both[size : size + 1], tail)
            tail = jnp.where(tail_row == 2 * pair + 1, diag, tail)
        return jnp.concatenate(bodies + [tail], axis=0)

    def pack_both(d, _):
        keep[d] = pack(d, core)
        send[d] = pack(d, 1 - core).astype(BF16)
        return 0

    lax.fori_loop(0, send.shape[0], pack_both, 0)


def scaled_grams(own, count, tile, block, turn, values, weight, members, tiles):
    blocks, size, rows = members.shape
    dests = tiles * ABLK // (CORES * own)
    shape = (dests, packed_rows(own), LANES)
    chunks = 4
    return pl.pallas_call(
        functools.partial(gram_kernel, own, chunks),
        out_shape=(jax.ShapeDtypeStruct(shape, BF16), jax.ShapeDtypeStruct(shape, F32)),
        in_specs=[scalars()] * 4 + [whole(), whole(), pl.BlockSpec(memory_space=pl.ANY)],
        out_specs=(whole(), whole()),
        scratch_shapes=[
            pltpu.VMEM((blocks, size, rows), BF16),
            pltpu.VMEM((tiles * ABLK, size + 8, LANES), F32),
            pltpu.SemaphoreType.DMA((chunks,)),
        ],
        compiler_params=pltpu.CompilerParams(vmem_limit_bytes=48 * 1024 * 1024),
        name="grams",
    )(count, tile, block, turn, values, weight, members)


def split(x):
    high = x.astype(BF16)
    return high, (x - high.astype(F32)).astype(BF16)


def left_of(x, first_half):
    high, low = split(x)
    return jnp.concatenate([high, jnp.where(first_half, low, jnp.zeros_like(low))], axis=1)


def right_of(x):
    high, low = split(x)
    return jnp.concatenate([high, low, high, high], axis=0)


def times(left, right):
    return jnp.dot(left, right, preferred_element_type=F32)


def transform_kernel(own, size, groups, arrived, weights_out, *rest):
    outs, spread = rest[:groups], rest[groups]
    summed = arrived[0].astype(F32)
    for s in range(1, arrived.shape[0]):
        summed = summed + arrived[s].astype(F32)
    half = size // 2
    col = iota((half, LANES), 1) % size
    row = iota((half, LANES), 0)
    upper = col >= half
    eye = (iota((size, LANES), 1) % size == iota((size, LANES), 0)).astype(F32)
    first_half = iota((size, LANES), 1) < size
    extra = 16 * own
    systems, projections = [], []
    for pair in range(own // 2):
        part = summed[half * pair : half * (pair + 1)]
        projection = summed[extra + 2 * pair : extra + 2 * pair + 1]
        diag = pltpu.roll(summed[extra : extra + 8], half, 1)[2 * pair + 1 : 2 * pair + 2]
        low = jnp.where(col < row, part, jnp.where(col == row, 0.5 * part, 0.0))
        top = jnp.where(upper, part, low)
        moved = pltpu.roll(part, half, 1)
        high = jnp.where(
            col - half > row, moved, jnp.where(col - half == row, 0.5 * diag, 0.0)
        )
        bottom = jnp.where(upper, high, 0.0)
        fold = jnp.concatenate([top, bottom], axis=0)
        turned = fold.T
        other = pltpu.roll(fold, size, 1)
        for t in range(2):
            here = turned[size * t : size * (t + 1)]
            here = jnp.concatenate([here, here], axis=1)
            one, two = (fold, other) if t == 0 else (other, fold)
            gram = jnp.where(first_half, one, two) + here
            systems.append((size - 1.0) * eye + gram)
            shifted = projection if t == 0 else pltpu.roll(
                jnp.broadcast_to(projection, (8, LANES)), size, 1
            )[:1]
            projections.append(shifted)
    inverse_frobs, roots, inverses = [], [], []
    for system in systems:
        squares = jnp.where(first_half, system * system, 0.0)
        frob = jnp.sqrt(jnp.sum(jnp.sum(squares, axis=0, keepdims=True), axis=1, keepdims=True))
        inverse_frobs.append(frob)
        roots.append(system / frob)
    for step in range(NS_STEPS):
        if step == 0:
            middles = [1.5 * eye - 0.5 * s for s in roots]
        else:
            middles = [
                1.5 * eye - 0.5 * times(left_of(z, first_half), right_of(s))
                for z, s in zip(inverses, roots)
            ]
        if step == 0:
            roots = [times(left_of(s, first_half), right_of(e)) for s, e in zip(roots, middles)]
            inverses = middles
        elif step < NS_STEPS - 1:
            stacked = [
                times(
                    jnp.concatenate([left_of(s, first_half), left_of(z, first_half)], axis=0),
                    right_of(e),
                )
                for s, z, e in zip(roots, inverses, middles)
            ]
            roots = [x[:size] for x in stacked]
            inverses = [x[size:] for x in stacked]
        else:
            inverses = [
                times(left_of(z, first_half), right_of(e)) for z, e in zip(inverses, middles)
            ]
    share = size // groups
    me = lax.axis_index("y") * CORES + lax.axis_index("core")
    rows8 = iota((8, LANES), 0)
    weights = jnp.zeros((8, LANES), F32)
    for q in range(own):
        inverse_root = inverses[q] / jnp.sqrt(inverse_frobs[q])
        spread[q] = jnp.sqrt(size - 1.0) * inverse_root
        moved = jnp.sum(
            jnp.where(first_half, inverse_root * projections[q], 0.0), axis=1, keepdims=True
        )
        mean_weights = jnp.sum(inverse_root * moved, axis=0, keepdims=True)
        weights = jnp.where(rows8 == q, mean_weights, weights)
    weights_out[...] = weights
    for b in range(groups):
        start = pl.multiple_of((me ^ b) * share, share)
        for q in range(own):
            outs[b][pl.ds(q * share, share), :] = spread[q, pl.ds(start, share), :].astype(BF16)


def transforms(own, size, groups, arrived):
    share = size // groups
    return pl.pallas_call(
        functools.partial(transform_kernel, own, size, groups),
        out_shape=(jax.ShapeDtypeStruct((8, LANES), F32),)
        + tuple(jax.ShapeDtypeStruct((own * share, LANES), BF16) for _ in range(groups)),
        in_specs=[whole()],
        out_specs=tuple([whole()] * (groups + 1)),
        scratch_shapes=[pltpu.VMEM((own, size, LANES), F32)],
        name="transforms",
    )(arrived)


def centre_kernel(own, *refs):
    groups = len(refs) - 2
    parts, pert, mean_out = refs[:groups], refs[groups], refs[groups + 1]
    share, ablk, width = parts[0].shape
    me = lax.axis_index("y") * CORES + lax.axis_index("core")
    size = share * groups
    step = 256

    def one(c, _):
        at = pl.ds(pl.multiple_of(c * step, step), step)
        total = jnp.zeros((ablk, step), F32)
        for part in parts:
            for i in range(share):
                total = total + part[i, :, at].astype(F32)
        mean = total / size
        mean_out[:, at] = mean
        for b, part in enumerate(parts):
            for i in range(share):
                pert[pl.ds((b * share + i) * ablk, ablk), at] = (
                    part[i, :, at].astype(F32) - mean
                ).astype(BF16)
        return 0

    lax.fori_loop(0, width // step, one, 0)


def centred(own, parts):
    share, ablk, width = parts[0].shape
    return pl.pallas_call(
        functools.partial(centre_kernel, own),
        out_shape=(
            jax.ShapeDtypeStruct((len(parts) * share * ablk, width), BF16),
            jax.ShapeDtypeStruct((ablk, width), F32),
        ),
        in_specs=[whole()] * len(parts),
        out_specs=(whole(), whole()),
        name="centre",
    )(*parts)


def apply_kernel(own, groups, weights, pert, mean, *refs):
    arrived, out_pert, out_mean = refs[:groups], refs[groups], refs[groups + 1]
    size_by_block, width = pert.shape
    share = arrived[0].shape[0] // own
    rows = share * ABLK
    me = lax.axis_index("y") * CORES + lax.axis_index("core")
    received = jnp.concatenate([r[...] for r in arrived], axis=0)
    per_source = own * share
    count = groups * per_source
    to_row = iota((rows, count), 0)
    from_row = iota((rows, count), 1)
    source = me ^ (from_row // per_source)
    within = from_row % per_source
    place = (to_row // ABLK == within % share) & (
        to_row % ABLK == source * own + within // share
    )
    spread = times(place.astype(F32).astype(BF16), received).astype(BF16)
    spread = jnp.concatenate([spread, weights[...].astype(BF16), jnp.zeros((8, LANES), BF16)], axis=0)
    column = iota((LANES, size_by_block), 1)
    member = (me ^ (column // (share * ABLK))) * share + (column // ABLK) % share
    repeat = (iota((LANES, size_by_block), 0) == member).astype(F32).astype(BF16)
    wide = times(spread, repeat)
    wide_row = iota(wide.shape, 0)
    block = jnp.where(wide_row < rows, wide_row % ABLK, me * own + wide_row - rows)
    wide = jnp.where(block == iota(wide.shape, 1) % ABLK, wide, 0.0).astype(BF16)
    step = 256
    for c in range(width // step):
        at = pl.ds(c * step, step)
        result = times(wide, pert[:, at])
        out_pert[:, at] = result[:rows].astype(BF16)
        means = mean[:, at]
        own_mean = means[:own]
        for m in range(1, groups):
            own_mean = jnp.where(me == m, means[m * own : (m + 1) * own], own_mean)
        out_mean[:, at] = (own_mean + result[rows : rows + own]).astype(BF16)


def applied(own, weights, pert, mean, arrived):
    groups = len(arrived)
    share = arrived[0].shape[0] // own
    width = pert.shape[1]
    return pl.pallas_call(
        functools.partial(apply_kernel, own, groups),
        out_shape=(
            jax.ShapeDtypeStruct((share * ABLK, width), BF16),
            jax.ShapeDtypeStruct((own, width), BF16),
        ),
        in_specs=[whole()] * (3 + groups),
        out_specs=(whole(), whole()),
        name="apply",
    )(weights, pert, mean, *arrived)


def body(ensemble, obs_members, obs_values, obs_weight, obs_count, obs_tile, obs_block, obs_turn):
    tiles = lax.axis_size("tile")
    rows_y = lax.axis_size("y")
    groups = rows_y * CORES
    own = ABLK // groups
    size = obs_members.shape[1]
    across = [(i, i ^ 1) for i in range(CORES)]

    def swapped(x, b):
        pairs = [(i, i ^ b) for i in range(groups)]
        return lax.ppermute(x, ("y", "core"), pairs)

    parts = [ensemble, swapped(ensemble, 1)]
    for b in range(2, groups, 2):
        far = swapped(ensemble, b)
        parts += [far, lax.ppermute(far, "core", across)]
    send, keep = scaled_grams(
        own, obs_count, obs_tile, obs_block, obs_turn, obs_values, obs_weight, obs_members, tiles
    )
    got = lax.ppermute(send, "core", across)
    mine = (keep + got.astype(F32)).astype(BF16)
    arrived = lax.all_to_all(mine, ("tile", "y"), split_axis=0, concat_axis=0, tiled=True)
    pert, mean = centred(own, parts)
    weights, *spreads = transforms(own, size, groups, arrived)
    spreads = [spreads[0]] + [swapped(s, b) for b, s in enumerate(spreads) if b]
    analysis_pert, analysis_mean = applied(own, weights, pert, mean, spreads)
    return analysis_pert.reshape(ensemble.shape), analysis_mean


def solution(mesh):
    tiles, groups = mesh.shape["tile"], mesh.shape["mem"]
    fine = Mesh(mesh.devices.reshape(tiles, groups // CORES, CORES), ("tile", "y", "core"))
    everyone = ("tile", "y", "core")
    placed = (
        P(("y", "core"), "tile", None),
        P(everyone, None, None),
        P(everyone, None),
        P(everyone, None),
        P(everyone),
        P(everyone),
        P(everyone),
        P(everyone),
    )
    return jax.shard_map(
        body,
        mesh=fine,
        in_specs=placed,
        out_specs=(P(("y", "core"), "tile", None), P(everyone, None)),
        check_vma=False,
    )
```

time: 201 us -> 54.7 us (0.27)
  waiting for transfers between devices: 86.4 us -> 10.9 us
  local copies, waits for them, and re-layouts: 36 us -> 8.77 us
  matrix products: 26.9 us -> 0 us
  Pallas kernels: 0 us -> 21.1 us
  between operations: 14.4 us -> 0.73 us
  other arithmetic: 11.5 us -> 0.77 us
  starting transfers between devices: 19.2 us -> 11.9 us
  blocking collectives: 5.93 us -> 0 us
    all_to_all x3 -> x1, waiting for transfers between devices: 46.4 us -> 4.17 us  [body(): lax.all_to_all(mine, ('tile', 'y'), split_axis=0, concat_axis=0, tiled=True)]
    dot_general x25 -> x0, matrix products: 26.9 us -> none  [the longest x18 12.7 us: product(): return jnp.matmul(left, right, precision=lax.Precision.HIGHEST)]
    psum x1 -> x0, waiting for transfers between devices: 26.9 us -> none  [body(): member_total = lax.psum(jnp.sum(ensemble, axis=0, dtype=jnp.float32), 'mem')]
    pallas_call x0 -> x4, Pallas kernels: none -> 21.1 us  [the longest x1 10.1 us: scaled_grams(): pl.pallas_call(functools.partial(gram_kernel, own, chunks), out_shape=(ja...]
    gather x2 -> x0, local copies, waits for them, and re-layouts: 20 us -> none  [the longest x1 16.1 us: body(): jnp.take(got_packed, jnp.asarray(lookup), axis=1)]
    all_gather x1 -> x0, waiting for transfers between devices: 13 us -> none  [body(): shard_rows = lax.all_gather(perturbation, 'mem', axis=0, tiled=True)]
    all_to_all x3 -> x1, starting transfers between devices: 19.1 us -> 6.84 us  [body(): lax.all_to_all(mine, ('tile', 'y'), split_axis=0, concat_axis=0, tiled=True)]
    ppermute x0 -> x7, waiting for transfers between devices: none -> 6.74 us  [the longest x5 6.74 us: swapped(): return lax.ppermute(x, ('y', 'core'), pairs)]
  transfers between devices with their start and end apart: 5 -> 8, of which waited for: 4 -> 2; matrix products, arithmetic and copies ran while one was open for 17% -> 1% of each run, Pallas kernels for 0% -> 14%
where the time goes in v1:
time: 54.7 us; the launch traced here: 54.2 us
  Pallas kernels  21.1 us (39%)
  starting transfers between devices  11.9 us (22%)
  waiting for transfers between devices  10.9 us (20%)
  local copies, waits for them, and re-layouts  8.77 us (16%)
  other arithmetic  0.77 us (1%)
  between operations  0.73 us (1%)
    pallas_call x1, Pallas kernels, scaled_grams(): pl.pallas_call(functools.partial(gram_kernel, own, chunks), out_shape=(ja...  10.1 us
    unnamed x30, local copies, waits for them, and re-layouts  8.77 us
    all_to_all x1, starting transfers between devices, body(): lax.all_to_all(mine, ('tile', 'y'), split_axis=0, concat_axis=0, tiled=True)  6.84 us
    ppermute x5, waiting for transfers between devices, swapped(): return lax.ppermute(x, ('y', 'core'), pairs)  6.74 us
    ppermute x5, starting transfers between devices, swapped(): return lax.ppermute(x, ('y', 'core'), pairs)  4.53 us
    all_to_all x1, waiting for transfers between devices, body(): lax.all_to_all(mine, ('tile', 'y'), split_axis=0, concat_axis=0, tiled=True)  4.17 us
    pallas_call x1, Pallas kernels, centred(): pl.pallas_call(functools.partial(centre_kernel, own), out_shape=(jax.Shap...  3.81 us
    pallas_call x1, Pallas kernels, transforms(): pl.pallas_call(functools.partial(transform_kernel, own, size, groups), ou...  3.74 us
  transfers between devices with their start and end apart: 8, of which 2 were waited for; matrix products, arithmetic and copies ran while one was open for 1% of the time, Pallas kernels for 14%

profile of v1, /device:TPU:0, one launch (start us, length us, event | category | flops | bytes accessed | tf_op | source)
XLA Modules:
  0.0 54.2 jit_solution(4289865758352910805)
XLA Ops:
  0.6 1.6 %copy-done = bf16[128,64,128]{2,1,0:T(8,128)(2,1)S(1)} copy-done((bf16[128,64,128]{2,1,0:T(8,128)(2,1)S(1)}, bf16[128,64,128]{2,1,0:T(8,128)(2,1)}, u32[]{:S(2)}) %copy-start) | copy-done | bytes 2097176
  2.2 0.8 %copy-done.1 = f32[128,128]{1,0:T(8,128)S(1)} copy-done((f32[128,128]{1,0:T(8,128)S(1)}, f32[128,128]{1,0:T(8,128)}, u32[]{:S(2)}) %copy-start.1) | copy-done | bytes 65560
  3.1 0.8 %copy-done.2 = f32[128,128]{1,0:T(8,128)S(1)} copy-done((f32[128,128]{1,0:T(8,128)S(1)}, f32[128,128]{1,0:T(8,128)}, u32[]{:S(2)}) %copy-start.2) | copy-done | bytes 65560
  3.9 0.7 %copy-done.3 = s32[128]{0:T(128)S(1)} copy-done((s32[128]{0:T(128)S(1)}, s32[128]{0:T(128)}, u32[]{:S(2)}) %copy-start.3) | copy-done | bytes 536
  4.6 0.7 %copy-done.4 = s32[128]{0:T(128)S(1)} copy-done((s32[128]{0:T(128)S(1)}, s32[128]{0:T(128)}, u32[]{:S(2)}) %copy-start.4) | copy-done | bytes 536
  5.2 0.7 %copy-done.5 = s32[128]{0:T(128)S(1)} copy-done((s32[128]{0:T(128)S(1)}, s32[128]{0:T(128)}, u32[]{:S(2)}) %copy-start.5) | copy-done | bytes 536
  5.9 0.7 %copy-done.6 = s32[128]{0:T(128)S(1)} copy-done((s32[128]{0:T(128)S(1)}, s32[128]{0:T(128)}, u32[]{:S(2)}) %copy-start.6) | copy-done | bytes 536
  6.5 10.1 %grams.1 = (bf16[16,72,128]{2,1,0:T(8,128)(2,1)S(1)}, f32[16,72,128]{2,1,0:T(8,128)S(1)}) custom-call(s32[128]{0:T(128)S(1)} %copy-done.3, s32[128]{0:T(128)S(1)} %copy-done.4, s32[128]{0:T(128)S(1)} %copy-done.5, s32[128]{0:T(128)S(1)} %copy-done.6, f32[128,128]{1,0:T(8,128)S(1)} %copy-done.1, f32[128,128]{1,0:T(8,128)S(1)} %copy-done.2, ...), custom_call_target="tpu_custom_call" | custom-call | tf_op jit(solution)/shard_map/grams/pallas_call | solution.py:128
  16.7 0.6 %collective-permute-start = (bf16[16,72,128]{2,1,0:T(8,128)(2,1)S(1)}, bf16[16,72,128]{2,1,0:T(8,128)(2,1)S(1)}, u32[]{:S(2)}, u32[]{:S(2)}) collective-permute-start(bf16[16,72,128]{2,1,0:T(8,128)(2,1)S(1)} %get-tuple-element.14), channel_id=1, source_target_pairs={{0,1},{1,0},{2,3},{3,2},{4,5},{5,4},{6,7},{7,6},{8,9},{9,8},{10,11... | collective-permute-start | bytes 884744 | tf_op jit(solution)/shard_map/ppermute | solution.py:374
  17.2 2.6 %collective-permute-start.2 = (bf16[16,16,1024]{2,1,0:T(8,128)(2,1)S(1)}, bf16[16,16,1024]{2,1,0:T(8,128)(2,1)S(1)}, u32[]{:S(2)}, u32[]{:S(2)}) collective-permute-start(bf16[16,16,1024]{2,1,0:T(8,128)(2,1)S(1)} %copy-done.8), channel_id=1, source_target_pairs={{0,2},{1,3},{2,0},{3,1},{4,6},{5,7},{6,4},{7,5},{8,10},{9,11},{10,... | collective-permute-start | bytes 1572872 | tf_op jit(solution)/shard_map/ppermute | solution.py:365
  19.8 0.8 %add_convert_fusion = bf16[16,72,128]{2,1,0:T(8,128)(2,1)} fusion(f32[16,72,128]{2,1,0:T(8,128)S(1)} %get-tuple-element.13, bf16[16,72,128]{2,1,0:T(8,128)(2,1)S(1)} %collective-permute-done), kind=kLoop, calls=%fused_computation | loop fusion | flops 442368 | bytes 1179648 | tf_op jit(solution)/shard_map/convert_element_type | solution.py:375
  20.6 6.8 %all-to-all-start = ((bf16[16,72,128]{2,1,0:T(8,128)(2,1)}), bf16[16,72,128]{2,1,0:T(8,128)(2,1)S(1)}, u32[]{:S(2)}, u32[]{:S(2)}) async-start(bf16[16,72,128]{2,1,0:T(8,128)(2,1)} %add_convert_fusion), calls=%async_computation | async-start | bytes 589824 | tf_op jit(solution)/shard_map/all_to_all | solution.py:376
  27.5 0.1 collective-permute-start.1
  27.5 6.7 %collective-permute-done.2.refs_2_ = bf16[16,16,1024]{2,1,0:T(8,128)(2,1)S(1)} collective-permute-done((bf16[16,16,1024]{2,1,0:T(8,128)(2,1)S(1)}, bf16[16,16,1024]{2,1,0:T(8,128)(2,1)S(1)}, u32[]{:S(2)}, u32[]{:S(2)}) %collective-permute-start.2) | collective-permute-done | bytes 524320 | tf_op jit(solution)/shard_map/ppermute | solution.py:365
  34.3 4.2 %all-to-all-done.arrived = bf16[16,72,128]{2,1,0:T(8,128)(2,1)S(1)} async-done(((bf16[16,72,128]{2,1,0:T(8,128)(2,1)}), bf16[16,72,128]{2,1,0:T(8,128)(2,1)S(1)}, u32[]{:S(2)}, u32[]{:S(2)}) %all-to-all-start) | async-done | bytes 294944 | tf_op jit(solution)/shard_map/all_to_all | solution.py:376
  38.4 0.7 %copy-done.7 = bf16[16,72,128]{2,1,0:T(8,128)(2,1)} copy-done((bf16[16,72,128]{2,1,0:T(8,128)(2,1)}, bf16[16,72,128]{2,1,0:T(8,128)(2,1)S(1)}, u32[]{:S(2)}) %copy-start.7) | copy-done | bytes 294936
  39.2 3.7 %transforms.1 = (f32[8,128]{1,0:T(8,128)}, bf16[64,128]{1,0:T(8,128)(2,1)}, bf16[64,128]{1,0:T(8,128)(2,1)}, bf16[64,128]{1,0:T(8,128)(2,1)}, bf16[64,128]{1,0:T(8,128)(2,1)}) custom-call(bf16[16,72,128]{2,1,0:T(8,128)(2,1)} %copy-done.7), custom_call_target="tpu_custom_call" | custom-call | tf_op jit(solution)/shard_map/transforms/pallas_call | solution.py:251
  42.9 0.6 %collective-permute-start.5 = (bf16[64,128]{1,0:T(8,128)(2,1)}, bf16[64,128]{1,0:T(8,128)(2,1)S(1)}, u32[]{:S(2)}, u32[]{:S(2)}) collective-permute-start(bf16[64,128]{1,0:T(8,128)(2,1)} %get-tuple-element.20), channel_id=1, source_target_pairs={{0,2},{1,3},{2,0},{3,1},{4,6},{5,7},{6,4},{7,5},{8,10},{9,11},{10,... | collective-permute-start | bytes 49160 | tf_op jit(solution)/shard_map/ppermute | solution.py:365
  43.5 1.3 %collective-permute-start.6 = (bf16[64,128]{1,0:T(8,128)(2,1)}, bf16[64,128]{1,0:T(8,128)(2,1)S(1)}, u32[]{:S(2)}, u32[]{:S(2)}) collective-permute-start(bf16[64,128]{1,0:T(8,128)(2,1)} %get-tuple-element.21), channel_id=1, source_target_pairs={{0,3},{1,2},{2,1},{3,0},{4,7},{5,6},{6,5},{7,4},{8,11},{9,10},{10,... | collective-permute-start | bytes 49160 | tf_op jit(solution)/shard_map/ppermute | solution.py:365
  44.8 0.8 %copy-done.10 = bf16[16,16,1024]{2,1,0:T(8,128)(2,1)} copy-done((bf16[16,16,1024]{2,1,0:T(8,128)(2,1)}, bf16[16,16,1024]{2,1,0:T(8,128)(2,1)S(1)}, u32[]{:S(2)}) %copy-start.10) | copy-done | bytes 524312
  45.6 0.8 %copy-done.11 = bf16[16,16,1024]{2,1,0:T(8,128)(2,1)} copy-done((bf16[16,16,1024]{2,1,0:T(8,128)(2,1)}, bf16[16,16,1024]{2,1,0:T(8,128)(2,1)S(1)}, u32[]{:S(2)}) %copy-start.11) | copy-done | bytes 524312
  46.4 3.8 %centre.1 = (bf16[1024,1024]{1,0:T(8,128)(2,1)}, f32[16,1024]{1,0:T(8,128)}) custom-call(bf16[16,16,1024]{2,1,0:T(8,128)(2,1)} %refs_0_.1, bf16[16,16,1024]{2,1,0:T(8,128)(2,1)} %copy-done.10, bf16[16,16,1024]{2,1,0:T(8,128)(2,1)} %copy-done.9, bf16[16,16,1024]{2,1,0:T(8,128)(2,1)} %copy-done.11), custom_call_target="tpu_custom_call" | custom-call | tf_op jit(solution)/shard_map/centre/pallas_call | solution.py:290
  50.2 0.6 %copy-done.12 = bf16[64,128]{1,0:T(8,128)(2,1)} copy-done((bf16[64,128]{1,0:T(8,128)(2,1)}, bf16[64,128]{1,0:T(8,128)(2,1)S(1)}, u32[]{:S(2)}) %copy-start.12) | copy-done | bytes 16408
  50.8 3.4 %apply.1 = (bf16[256,1024]{1,0:T(8,128)(2,1)}, bf16[4,1024]{1,0:T(4,128)(2,1)}) custom-call(f32[8,128]{1,0:T(8,128)} %get-tuple-element.15.weights, bf16[1024,1024]{1,0:T(8,128)(2,1)} %get-tuple-element.16.pert, f32[16,1024]{1,0:T(8,128)} %get-tuple-element.17.mean, bf16[64,128]{1,0:T(8,128)(2,1)} %get-tuple-element.18.refs_0_, bf16[64,128]{1,0:T(8,128)(2,1)} %copy-done.12, ...), custom_call_target="tpu_custom_call" | custom-call | tf_op jit(solution)/shard_map/apply/pallas_call | solution.py:343
  (27 shorter events, 0.1 us)
Async XLA Ops:
  0.6 1.6 %copy-start = (bf16[128,64,128]{2,1,0:T(8,128)(2,1)S(1)}, bf16[128,64,128]{2,1,0:T(8,128)(2,1)}, u32[]{:S(2)}) copy-start(bf16[128,64,128]{2,1,0:T(8,128)(2,1)} %members_hbm.1) | copy-start | bytes 6291460
  2.2 0.8 %copy-start.1 = (f32[128,128]{1,0:T(8,128)S(1)}, f32[128,128]{1,0:T(8,128)}, u32[]{:S(2)}) copy-start(f32[128,128]{1,0:T(8,128)} %values.1) | copy-start | bytes 196612
  3.1 0.8 %copy-start.2 = (f32[128,128]{1,0:T(8,128)S(1)}, f32[128,128]{1,0:T(8,128)}, u32[]{:S(2)}) copy-start(f32[128,128]{1,0:T(8,128)} %weight.1) | copy-start | bytes 196612
  3.9 0.7 %copy-start.3 = (s32[128]{0:T(128)S(1)}, s32[128]{0:T(128)}, u32[]{:S(2)}) copy-start(s32[128]{0:T(128)} %count.1) | copy-start | bytes 1540
  4.6 0.7 %copy-start.4 = (s32[128]{0:T(128)S(1)}, s32[128]{0:T(128)}, u32[]{:S(2)}) copy-start(s32[128]{0:T(128)} %tile.1) | copy-start | bytes 1540
  5.2 0.7 %copy-start.5 = (s32[128]{0:T(128)S(1)}, s32[128]{0:T(128)}, u32[]{:S(2)}) copy-start(s32[128]{0:T(128)} %block.1) | copy-start | bytes 1540
  5.9 0.7 %copy-start.6 = (s32[128]{0:T(128)S(1)}, s32[128]{0:T(128)}, u32[]{:S(2)}) copy-start(s32[128]{0:T(128)} %turn.1) | copy-start | bytes 1540
  6.5 10.7 %copy-start.8 = (bf16[16,16,1024]{2,1,0:T(8,128)(2,1)S(1)}, bf16[16,16,1024]{2,1,0:T(8,128)(2,1)}, u32[]{:S(2)}) copy-start(bf16[16,16,1024]{2,1,0:T(8,128)(2,1)} %refs_0_.1) | copy-start | bytes 1572868
  16.7 3.2 %collective-permute-start = (bf16[16,72,128]{2,1,0:T(8,128)(2,1)S(1)}, bf16[16,72,128]{2,1,0:T(8,128)(2,1)S(1)}, u32[]{:S(2)}, u32[]{:S(2)}) collective-permute-start(bf16[16,72,128]{2,1,0:T(8,128)(2,1)S(1)} %get-tuple-element.14), channel_id=1, source_target_pairs={{0,1},{1,0},{2,3},{3,2},{4,5},{5,4},{6,7},{7,6},{8,9},{9,8},{10,11... | collective-permute-start | bytes 884744 | tf_op jit(solution)/shard_map/ppermute | solution.py:374
  17.2 17.0 %collective-permute-start.2 = (bf16[16,16,1024]{2,1,0:T(8,128)(2,1)S(1)}, bf16[16,16,1024]{2,1,0:T(8,128)(2,1)S(1)}, u32[]{:S(2)}, u32[]{:S(2)}) collective-permute-start(bf16[16,16,1024]{2,1,0:T(8,128)(2,1)S(1)} %copy-done.8), channel_id=1, source_target_pairs={{0,2},{1,3},{2,0},{3,1},{4,6},{5,7},{6,4},{7,5},{8,10},{9,11},{10,... | collective-permute-start | bytes 1572872 | tf_op jit(solution)/shard_map/ppermute | solution.py:365
  20.6 17.8 %all-to-all-start = ((bf16[16,72,128]{2,1,0:T(8,128)(2,1)}), bf16[16,72,128]{2,1,0:T(8,128)(2,1)S(1)}, u32[]{:S(2)}, u32[]{:S(2)}) async-start(bf16[16,72,128]{2,1,0:T(8,128)(2,1)} %add_convert_fusion), calls=%async_computation | async-start | bytes 589824 | tf_op jit(solution)/shard_map/all_to_all | solution.py:376
  27.5 17.3 %collective-permute-start.1 = (bf16[16,16,1024]{2,1,0:T(8,128)(2,1)S(1)}, bf16[16,16,1024]{2,1,0:T(8,128)(2,1)S(1)}, u32[]{:S(2)}, u32[]{:S(2)}) collective-permute-start(bf16[16,16,1024]{2,1,0:T(8,128)(2,1)S(1)} %copy-done.8), channel_id=1, source_target_pairs={{0,1},{1,0},{2,3},{3,2},{4,5},{5,4},{6,7},{7,6},{8,9},{9,8},{10,11... | collective-permute-start | bytes 1572872 | tf_op jit(solution)/shard_map/ppermute | solution.py:365
  34.3 10.5 %copy-start.9 = (bf16[16,16,1024]{2,1,0:T(8,128)(2,1)}, bf16[16,16,1024]{2,1,0:T(8,128)(2,1)S(1)}, u32[]{:S(2)}) copy-start(bf16[16,16,1024]{2,1,0:T(8,128)(2,1)S(1)} %collective-permute-done.2.refs_2_) | copy-start | bytes 1572868
  34.3 10.5 %collective-permute-start.3 = (bf16[16,16,1024]{2,1,0:T(8,128)(2,1)S(1)}, bf16[16,16,1024]{2,1,0:T(8,128)(2,1)S(1)}, u32[]{:S(2)}, u32[]{:S(2)}) collective-permute-start(bf16[16,16,1024]{2,1,0:T(8,128)(2,1)S(1)} %collective-permute-done.2.refs_2_), channel_id=1, source_target_pairs={{0,1},{1,0},{2,3},{3,2},{4,5},{5,4},{6,7},{7,6},{8,9},{9,8},{10,11... | collective-permute-start | bytes 1572872 | tf_op jit(solution)/shard_map/ppermute | solution.py:370
  38.4 0.7 %copy-start.7 = (bf16[16,72,128]{2,1,0:T(8,128)(2,1)}, bf16[16,72,128]{2,1,0:T(8,128)(2,1)S(1)}, u32[]{:S(2)}) copy-start(bf16[16,72,128]{2,1,0:T(8,128)(2,1)S(1)} %all-to-all-done.arrived) | copy-start | bytes 884740
  42.9 7.3 %collective-permute-start.4 = (bf16[64,128]{1,0:T(8,128)(2,1)}, bf16[64,128]{1,0:T(8,128)(2,1)S(1)}, u32[]{:S(2)}, u32[]{:S(2)}) collective-permute-start(bf16[64,128]{1,0:T(8,128)(2,1)} %get-tuple-element.19), channel_id=1, source_target_pairs={{0,1},{1,0},{2,3},{3,2},{4,5},{5,4},{6,7},{7,6},{8,9},{9,8},{10,11... | collective-permute-start | bytes 49160 | tf_op jit(solution)/shard_map/ppermute | solution.py:365
  42.9 7.3 %collective-permute-start.5 = (bf16[64,128]{1,0:T(8,128)(2,1)}, bf16[64,128]{1,0:T(8,128)(2,1)S(1)}, u32[]{:S(2)}, u32[]{:S(2)}) collective-permute-start(bf16[64,128]{1,0:T(8,128)(2,1)} %get-tuple-element.20), channel_id=1, source_target_pairs={{0,2},{1,3},{2,0},{3,1},{4,6},{5,7},{6,4},{7,5},{8,10},{9,11},{10,... | collective-permute-start | bytes 49160 | tf_op jit(solution)/shard_map/ppermute | solution.py:365
  43.5 6.7 %collective-permute-start.6 = (bf16[64,128]{1,0:T(8,128)(2,1)}, bf16[64,128]{1,0:T(8,128)(2,1)S(1)}, u32[]{:S(2)}, u32[]{:S(2)}) collective-permute-start(bf16[64,128]{1,0:T(8,128)(2,1)} %get-tuple-element.21), channel_id=1, source_target_pairs={{0,3},{1,2},{2,1},{3,0},{4,7},{5,6},{6,5},{7,4},{8,11},{9,10},{10,... | collective-permute-start | bytes 49160 | tf_op jit(solution)/shard_map/ppermute | solution.py:365
  44.8 0.8 %copy-start.10 = (bf16[16,16,1024]{2,1,0:T(8,128)(2,1)}, bf16[16,16,1024]{2,1,0:T(8,128)(2,1)S(1)}, u32[]{:S(2)}) copy-start(bf16[16,16,1024]{2,1,0:T(8,128)(2,1)S(1)} %collective-permute-done.1.refs_1_) | copy-start | bytes 1572868
  45.6 0.8 %copy-start.11 = (bf16[16,16,1024]{2,1,0:T(8,128)(2,1)}, bf16[16,16,1024]{2,1,0:T(8,128)(2,1)S(1)}, u32[]{:S(2)}) copy-start(bf16[16,16,1024]{2,1,0:T(8,128)(2,1)S(1)} %collective-permute-done.3.refs_3_) | copy-start | bytes 1572868
  50.2 0.6 %copy-start.12 = (bf16[64,128]{1,0:T(8,128)(2,1)}, bf16[64,128]{1,0:T(8,128)(2,1)S(1)}, u32[]{:S(2)}) copy-start(bf16[64,128]{1,0:T(8,128)(2,1)S(1)} %collective-permute-done.4.refs_1_) | copy-start | bytes 49156
  50.2 0.6 %copy-start.13 = (bf16[64,128]{1,0:T(8,128)(2,1)}, bf16[64,128]{1,0:T(8,128)(2,1)S(1)}, u32[]{:S(2)}) copy-start(bf16[64,128]{1,0:T(8,128)(2,1)S(1)} %collective-permute-done.5.refs_2_) | copy-start | bytes 49156
  50.2 0.6 %copy-start.14 = (bf16[64,128]{1,0:T(8,128)(2,1)}, bf16[64,128]{1,0:T(8,128)(2,1)S(1)}, u32[]{:S(2)}) copy-start(bf16[64,128]{1,0:T(8,128)(2,1)S(1)} %collective-permute-done.6.refs_3_) | copy-start | bytes 49156

commit v2 on v1

--- a/solution.py
+++ b/solution.py
@@ -6,6 +6,7 @@
 from jax.experimental import pallas as pl
 from jax.experimental.pallas import tpu as pltpu
 from jax.sharding import Mesh, PartitionSpec as P
+
 
 BPS = 4
 ABLK = BPS * BPS
@@ -24,16 +25,12 @@
     return (16 * own + own + 7) // 8 * 8
 
 
-def whole(shape=None):
+def whole():
     return pl.BlockSpec(memory_space=pltpu.VMEM)
 
 
-def scalars():
-    return pl.BlockSpec(memory_space=pltpu.SMEM)
-
-
 def target_of(tile, block, turn):
-    row, col = block // BPS, block % BPS
+    row, col = block >> 2, block & 3
     last = BPS - 1
     new_row = jnp.where(
         turn == 0, row, jnp.where(turn == 1, col, jnp.where(turn == 2, last - row, last - col))
@@ -44,49 +41,70 @@
     return tile * ABLK + new_row * BPS + new_col
 
 
-def gram_kernel(
-    own, chunks, count, tile, block, turn, values, weight, members_hbm, send, keep, members, total, sems
-):
+def gram_kernel(own, chunks, *refs):
+    sources, (send, keep) = refs[:7], refs[7:9]
+    held, total, sems = refs[9:16], refs[16], refs[17]
+    count, tile, block, turn, values, weight, members = held
     blocks, size, rows = members.shape
     per_chunk = blocks // chunks
-    copies = [
-        pltpu.make_async_copy(
-            members_hbm.at[pl.ds(c * per_chunk, per_chunk)],
-            members.at[pl.ds(c * per_chunk, per_chunk)],
-            sems.at[c],
-        )
-        for c in range(chunks)
-    ]
-    for copy in copies:
+
+    def fetch(c):
+        at = pl.ds(pl.multiple_of(c * per_chunk, per_chunk), per_chunk)
+        return pltpu.make_async_copy(sources[6].at[at], members.at[at], sems.at[6 + c])
+
+    small = [pltpu.make_async_copy(sources[i], held[i], sems.at[i]) for i in range(6)]
+    for copy in small:
         copy.start()
+    for c in range(chunks):
+        fetch(c).start()
 
     def clear(t, _):
         total[t] = jnp.zeros(total.shape[1:], F32)
         return 0
 
     lax.fori_loop(0, total.shape[0], clear, 0, unroll=4)
+    for copy in small:
+        copy.wait()
     lane = iota((1, rows), 1)
-    first = iota((16, rows), 0) == 0
-
-    def add_block(n, _):
+    tail_row = iota((16, rows), 0)
+    in_first = iota((size, LANES), 1) < size
+    tail_first = in_first[:8] & (iota((8, LANES), 0) == 0)
+    tail_second = ~in_first[:8] & (iota((8, LANES), 0) == 1)
+
+    def scaled(n):
         perts = members[n].astype(F32)
         mean = jnp.sum(perts, axis=0, keepdims=True) / size
         root = jnp.sqrt(jnp.where(lane < count[n], weight[pl.ds(n, 1), :], 0.0))
-        scaled = ((perts - mean) * root).astype(BF16)
-        innov = (values[pl.ds(n, 1), :] - mean) * root
-        tail = jnp.where(first, innov, 0.0).astype(BF16)
-        left = jnp.concatenate([scaled, tail], axis=0)
-        right = jnp.concatenate([scaled, scaled], axis=0)
+        return ((perts - mean) * root).astype(BF16), (values[pl.ds(n, 1), :] - mean) * root
+
+    def add_pair(i):
+        one, innov_one = scaled(2 * i)
+        two, innov_two = scaled(2 * i + 1)
+        tail = jnp.where(tail_row == 0, innov_one, jnp.where(tail_row == 1, innov_two, 0.0))
+        right = jnp.concatenate([one, two], axis=0)
+        left = jnp.concatenate([one, two, tail.astype(BF16)], axis=0)
         products = lax.dot_general(
             left, right, (((1,), (1,)), ((), ())), preferred_element_type=F32
         )
-        t = target_of(tile[n], block[n], turn[n])
-        total[t] = total[t] + products[: size + 8]
+        ends = products[2 * size : 2 * size + 8]
+        t = target_of(tile[2 * i], block[2 * i], turn[2 * i])
+        total[t, :size] = total[t, :size] + jnp.where(in_first, products[:size], 0.0)
+        total[t, size:] = total[t, size:] + jnp.where(tail_first, ends, 0.0)
+        t = target_of(tile[2 * i + 1], block[2 * i + 1], turn[2 * i + 1])
+        total[t, :size] = total[t, :size] + jnp.where(in_first, 0.0, products[size : 2 * size])
+        total[t, size:] = total[t, size:] + jnp.where(tail_second, ends, 0.0)
         return 0
 
-    for c in range(chunks):
-        copies[c].wait()
-        lax.fori_loop(c * per_chunk, (c + 1) * per_chunk, add_block, 0, unroll=4)
+    def add_chunk(c, _):
+        fetch(c).wait()
+        half_chunk = per_chunk // 2
+
+        def step(i, _):
+            return add_pair(c * half_chunk + i)
+
+        return lax.fori_loop(0, half_chunk, step, 0, unroll=4)
+
+    lax.fori_loop(0, chunks, add_chunk, 0)
 
     half = size // 2
     lane_half = iota((half, LANES), 1)
@@ -94,22 +112,29 @@
     row = iota((half, LANES), 0)
     from_top = (col >= half) | (col <= row)
     on_diag = col == row
-    first_of_pair = iota((size + 8, LANES), 1) < size
     core = lax.axis_index("core")
-    tail_row = iota((8, LANES), 0)
+    row8 = iota((8, LANES), 0)
+
+    def halves_added(even, odd, mask):
+        one = jnp.where(mask, even, odd)
+        two = jnp.where(mask, odd, even)
+        return one, pltpu.roll(two, size, 1)
 
     def pack(d, side):
         base = d * (CORES * own) + side * own
         bodies = []
         tail = jnp.zeros((8, LANES), F32)
         for pair in range(own // 2):
-            both = jnp.where(first_of_pair, total[base + 2 * pair], total[base + 2 * pair + 1])
+            even, odd = base + 2 * pair, base + 2 * pair + 1
+            both = sum(halves_added(total[even, :size], total[odd, :size], in_first))
             top = both[:half]
             bottom = pltpu.roll(both[half:size], LANES - half, 1)
             bodies.append(jnp.where(from_top, top, bottom))
             diag = jnp.sum(jnp.where(on_diag, bottom, 0.0), axis=0, keepdims=True)
-            tail = jnp.where(tail_row == 2 * pair, both[size : size + 1], tail)
-            tail = jnp.where(tail_row == 2 * pair + 1, diag, tail)
+            one, two = halves_added(total[even, size:], total[odd, size:], in_first[:8])
+            projections = jnp.sum(one + two, axis=0, keepdims=True)
+            tail = jnp.where(row8 == 2 * pair, projections, tail)
+            tail = jnp.where(row8 == 2 * pair + 1, diag, tail)
         return jnp.concatenate(bodies + [tail], axis=0)
 
     def pack_both(d, _):
@@ -118,6 +143,14 @@
         return 0
 
     lax.fori_loop(0, send.shape[0], pack_both, 0)
+
+
+def hbm():
+    return pl.BlockSpec(memory_space=pltpu.HBM)
+
+
+def params(mib):
+    return pltpu.CompilerParams(vmem_limit_bytes=mib * 1024 * 1024)
 
 
 def scaled_grams(own, count, tile, block, turn, values, weight, members, tiles):
@@ -125,17 +158,20 @@
     dests = tiles * ABLK // (CORES * own)
     shape = (dests, packed_rows(own), LANES)
     chunks = 4
+    small = tiles * ABLK * (size + 8) * LANES * 4 // (1024 * 1024)
     return pl.pallas_call(
         functools.partial(gram_kernel, own, chunks),
         out_shape=(jax.ShapeDtypeStruct(shape, BF16), jax.ShapeDtypeStruct(shape, F32)),
-        in_specs=[scalars()] * 4 + [whole(), whole(), pl.BlockSpec(memory_space=pl.ANY)],
+        in_specs=[hbm()] * 7,
         out_specs=(whole(), whole()),
-        scratch_shapes=[
+        scratch_shapes=[pltpu.SMEM((blocks,), jnp.int32)] * 4
+        + [pltpu.VMEM((blocks, rows), F32)] * 2
+        + [
             pltpu.VMEM((blocks, size, rows), BF16),
             pltpu.VMEM((tiles * ABLK, size + 8, LANES), F32),
-            pltpu.SemaphoreType.DMA((chunks,)),
+            pltpu.SemaphoreType.DMA((6 + chunks,)),
         ],
-        compiler_params=pltpu.CompilerParams(vmem_limit_bytes=48 * 1024 * 1024),
+        compiler_params=params(small + 12),
         name="grams",
     )(count, tile, block, turn, values, weight, members)
 
@@ -255,15 +291,15 @@
         in_specs=[whole()],
         out_specs=tuple([whole()] * (groups + 1)),
         scratch_shapes=[pltpu.VMEM((own, size, LANES), F32)],
+        compiler_params=params(8),
         name="transforms",
     )(arrived)
 
 
-def centre_kernel(own, *refs):
+def centre_kernel(*refs):
     groups = len(refs) - 2
     parts, pert, mean_out = refs[:groups], refs[groups], refs[groups + 1]
     share, ablk, width = parts[0].shape
-    me = lax.axis_index("y") * CORES + lax.axis_index("core")
     size = share * groups
     step = 256
 
@@ -285,22 +321,23 @@
     lax.fori_loop(0, width // step, one, 0)
 
 
-def centred(own, parts):
+def centred(parts):
     share, ablk, width = parts[0].shape
     return pl.pallas_call(
-        functools.partial(centre_kernel, own),
+        centre_kernel,
         out_shape=(
             jax.ShapeDtypeStruct((len(parts) * share * ablk, width), BF16),
             jax.ShapeDtypeStruct((ablk, width), F32),
         ),
         in_specs=[whole()] * len(parts),
         out_specs=(whole(), whole()),
+        compiler_params=params(12),
         name="centre",
     )(*parts)
 
 
 def apply_kernel(own, groups, weights, pert, mean, *refs):
-    arrived, out_pert, out_mean = refs[:groups], refs[groups], refs[groups + 1]
+    arrived, out_pert, out_mean, staged, sems = refs[:groups], *refs[groups:]
     size_by_block, width = pert.shape
     share = arrived[0].shape[0] // own
     rows = share * ABLK
@@ -324,22 +361,28 @@
     wide_row = iota(wide.shape, 0)
     block = jnp.where(wide_row < rows, wide_row % ABLK, me * own + wide_row - rows)
     wide = jnp.where(block == iota(wide.shape, 1) % ABLK, wide, 0.0).astype(BF16)
-    step = 256
+    step = staged.shape[2]
+    copies = []
     for c in range(width // step):
         at = pl.ds(c * step, step)
         result = times(wide, pert[:, at])
-        out_pert[:, at] = result[:rows].astype(BF16)
+        staged[c] = result[:rows].astype(BF16)
+        copies.append(pltpu.make_async_copy(staged.at[c], out_pert.at[:, at], sems.at[c]))
+        copies[-1].start()
         means = mean[:, at]
         own_mean = means[:own]
         for m in range(1, groups):
             own_mean = jnp.where(me == m, means[m * own : (m + 1) * own], own_mean)
         out_mean[:, at] = (own_mean + result[rows : rows + own]).astype(BF16)
+    for copy in copies:
+        copy.wait()
 
 
 def applied(own, weights, pert, mean, arrived):
     groups = len(arrived)
     share = arrived[0].shape[0] // own
     width = pert.shape[1]
+    step = 256
     return pl.pallas_call(
         functools.partial(apply_kernel, own, groups),
         out_shape=(
@@ -347,15 +390,19 @@
             jax.ShapeDtypeStruct((own, width), BF16),
         ),
         in_specs=[whole()] * (3 + groups),
-        out_specs=(whole(), whole()),
+        out_specs=(hbm(), whole()),
+        scratch_shapes=[
+            pltpu.VMEM((width // step, share * ABLK, step), BF16),
+            pltpu.SemaphoreType.DMA((width // step,)),
+        ],
+        compiler_params=params(16),
         name="apply",
     )(weights, pert, mean, *arrived)
 
 
 def body(ensemble, obs_members, obs_values, obs_weight, obs_count, obs_tile, obs_block, obs_turn):
     tiles = lax.axis_size("tile")
-    rows_y = lax.axis_size("y")
-    groups = rows_y * CORES
+    groups = lax.axis_size("y") * CORES
     own = ABLK // groups
     size = obs_members.shape[1]
     across = [(i, i ^ 1) for i in range(CORES)]
@@ -364,17 +411,19 @@
         pairs = [(i, i ^ b) for i in range(groups)]
         return lax.ppermute(x, ("y", "core"), pairs)
 
-    parts = [ensemble, swapped(ensemble, 1)]
-    for b in range(2, groups, 2):
-        far = swapped(ensemble, b)
-        parts += [far, lax.ppermute(far, "core", across)]
+    far = [swapped(ensemble, b) for b in range(2, groups, 2)]
+    near = swapped(ensemble, 1)
     send, keep = scaled_grams(
-        own, obs_count, obs_tile, obs_block, obs_turn, obs_values, obs_weight, obs_members, tiles
+        own, obs_count, obs_tile, obs_block, obs_turn, obs_values, obs_weight,
+        obs_members, tiles,
     )
     got = lax.ppermute(send, "core", across)
     mine = (keep + got.astype(F32)).astype(BF16)
     arrived = lax.all_to_all(mine, ("tile", "y"), split_axis=0, concat_axis=0, tiled=True)
-    pert, mean = centred(own, parts)
+    parts = [ensemble, near]
+    for x in far:
+        parts += [x, lax.ppermute(x, "core", across)]
+    pert, mean = centred(parts)
     weights, *spreads = transforms(own, size, groups, arrived)
     spreads = [spreads[0]] + [swapped(s, b) for b, s in enumerate(spreads) if b]
     analysis_pert, analysis_mean = applied(own, weights, pert, mean, spreads)

time: 54.7 us -> 45.1 us (0.82)
  Pallas kernels: 21.1 us -> 13.3 us
  local copies, waits for them, and re-layouts: 8.77 us -> 5.88 us
  waiting for transfers between devices: 10.9 us -> 12.1 us
    unnamed x30 -> x16, local copies, waits for them, and re-layouts: 8.77 us -> 5.88 us
    pallas_call x1, Pallas kernels: 3.81 us -> 0.93 us  [centred(): pl.pallas_call(centre_kernel, out_shape=(jax.ShapeDtypeStruct((len(parts)...]
    pallas_call x1, Pallas kernels: 10.1 us -> 7.84 us  [scaled_grams(): pl.pallas_call(functools.partial(gram_kernel, own, chunks), out_shape=(ja...]
    pallas_call x1, Pallas kernels: 3.74 us -> 2.18 us  [transforms(): pl.pallas_call(functools.partial(transform_kernel, own, size, groups), ou...]
    pallas_call x1, Pallas kernels: 3.39 us -> 2.35 us  [applied(): pl.pallas_call(functools.partial(apply_kernel, own, groups), out_shape=(j...]
    ppermute x5, waiting for transfers between devices: 6.74 us -> 7.55 us  [swapped(): return lax.ppermute(x, ('y', 'core'), pairs)]
  transfers between devices with their start and end apart: 8 -> 8, of which waited for: 2 -> 3; matrix products, arithmetic and copies ran while one was open for 1% -> 2% of each run, Pallas kernels for 14% -> 7%
where the time goes in v2:
time: 45.1 us; the launch traced here: 44.7 us
  Pallas kernels  13.3 us (29%)
  waiting for transfers between devices  12.1 us (27%)
  starting transfers between devices  12 us (27%)
  local copies, waits for them, and re-layouts  5.88 us (13%)
  other arithmetic  0.78 us (2%)
  between operations  0.71 us (2%)
    pallas_call x1, Pallas kernels, scaled_grams(): pl.pallas_call(functools.partial(gram_kernel, own, chunks), out_shape=(ja...  7.84 us
    ppermute x5, waiting for transfers between devices, swapped(): return lax.ppermute(x, ('y', 'core'), pairs)  7.55 us
    all_to_all x1, starting transfers between devices, body(): lax.all_to_all(mine, ('tile', 'y'), split_axis=0, concat_axis=0, tiled=True)  6.83 us
    unnamed x16, local copies, waits for them, and re-layouts  5.88 us
    ppermute x5, starting transfers between devices, swapped(): return lax.ppermute(x, ('y', 'core'), pairs)  4.58 us
    all_to_all x1, waiting for transfers between devices, body(): lax.all_to_all(mine, ('tile', 'y'), split_axis=0, concat_axis=0, tiled=True)  4.52 us
    pallas_call x1, Pallas kernels, applied(): pl.pallas_call(functools.partial(apply_kernel, own, groups), out_shape=(j...  2.35 us
    pallas_call x1, Pallas kernels, transforms(): pl.pallas_call(functools.partial(transform_kernel, own, size, groups), ou...  2.18 us
  transfers between devices with their start and end apart: 8, of which 3 were waited for; matrix products, arithmetic and copies ran while one was open for 2% of the time, Pallas kernels for 7%

profile of v2, /device:TPU:0, one launch (start us, length us, event | category | flops | bytes accessed | tf_op | source)
XLA Modules:
  0.0 44.7 jit_solution(10956017390731090755)
XLA Ops:
  0.6 1.6 %copy-done = bf16[128,64,128]{2,1,0:T(8,128)(2,1)S(1)} copy-done((bf16[128,64,128]{2,1,0:T(8,128)(2,1)S(1)}, bf16[128,64,128]{2,1,0:T(8,128)(2,1)}, u32[]{:S(2)}) %copy-start) | copy-done | bytes 2097176
  2.2 0.8 %copy-done.2 = f32[128,128]{1,0:T(8,128)S(1)} copy-done((f32[128,128]{1,0:T(8,128)S(1)}, f32[128,128]{1,0:T(8,128)}, u32[]{:S(2)}) %copy-start.2) | copy-done | bytes 65560
  3.1 0.8 %copy-done.3 = f32[128,128]{1,0:T(8,128)S(1)} copy-done((f32[128,128]{1,0:T(8,128)S(1)}, f32[128,128]{1,0:T(8,128)}, u32[]{:S(2)}) %copy-start.3) | copy-done | bytes 65560
  3.9 0.7 %copy-done.4 = s32[128]{0:T(128)S(1)} copy-done((s32[128]{0:T(128)S(1)}, s32[128]{0:T(128)}, u32[]{:S(2)}) %copy-start.4) | copy-done | bytes 536
  4.6 0.7 %copy-done.5 = s32[128]{0:T(128)S(1)} copy-done((s32[128]{0:T(128)S(1)}, s32[128]{0:T(128)}, u32[]{:S(2)}) %copy-start.5) | copy-done | bytes 536
  5.2 0.7 %copy-done.6 = s32[128]{0:T(128)S(1)} copy-done((s32[128]{0:T(128)S(1)}, s32[128]{0:T(128)}, u32[]{:S(2)}) %copy-start.6) | copy-done | bytes 536
  5.9 0.7 %copy-done.7 = s32[128]{0:T(128)S(1)} copy-done((s32[128]{0:T(128)S(1)}, s32[128]{0:T(128)}, u32[]{:S(2)}) %copy-start.7) | copy-done | bytes 536
  6.5 7.8 %grams.1 = (bf16[16,72,128]{2,1,0:T(8,128)(2,1)S(1)}, f32[16,72,128]{2,1,0:T(8,128)S(1)}) custom-call(s32[128]{0:T(128)S(1)} %copy-done.4, s32[128]{0:T(128)S(1)} %copy-done.5, s32[128]{0:T(128)S(1)} %copy-done.6, s32[128]{0:T(128)S(1)} %copy-done.7, f32[128,128]{1,0:T(8,128)S(1)} %copy-done.2, f32[128,128]{1,0:T(8,128)S(1)} %copy-done.3, ...), custom_call_target="tpu_custom_call" | custom-call | tf_op jit(solution)/shard_map/grams/pallas_call | solution.py:162
  14.4 0.6 %collective-permute-start = (bf16[16,72,128]{2,1,0:T(8,128)(2,1)S(1)}, bf16[16,72,128]{2,1,0:T(8,128)(2,1)S(1)}, u32[]{:S(2)}, u32[]{:S(2)}) collective-permute-start(bf16[16,72,128]{2,1,0:T(8,128)(2,1)S(1)} %get-tuple-element.14), channel_id=1, source_target_pairs={{0,1},{1,0},{2,3},{3,2},{4,5},{5,4},{6,7},{7,6},{8,9},{9,8},{10,11... | collective-permute-start | bytes 884744 | tf_op jit(solution)/shard_map/ppermute | solution.py:420
  14.9 2.6 %collective-permute-start.2 = (bf16[16,16,1024]{2,1,0:T(8,128)(2,1)S(1)}, bf16[16,16,1024]{2,1,0:T(8,128)(2,1)S(1)}, u32[]{:S(2)}, u32[]{:S(2)}) collective-permute-start(bf16[16,16,1024]{2,1,0:T(8,128)(2,1)S(1)} %copy-done.1), channel_id=1, source_target_pairs={{0,2},{1,3},{2,0},{3,1},{4,6},{5,7},{6,4},{7,5},{8,10},{9,11},{10,... | collective-permute-start | bytes 1572872 | tf_op jit(solution)/shard_map/ppermute | solution.py:412
  17.5 0.0 collective-permute-done
  17.5 0.8 %add_convert_fusion = bf16[16,72,128]{2,1,0:T(8,128)(2,1)} fusion(f32[16,72,128]{2,1,0:T(8,128)S(1)} %get-tuple-element.13, bf16[16,72,128]{2,1,0:T(8,128)(2,1)S(1)} %collective-permute-done), kind=kLoop, calls=%fused_computation | loop fusion | flops 442368 | bytes 1179648 | tf_op jit(solution)/shard_map/convert_element_type | solution.py:421
  18.3 6.8 %all-to-all-start = ((bf16[16,72,128]{2,1,0:T(8,128)(2,1)}), bf16[16,72,128]{2,1,0:T(8,128)(2,1)S(1)}, u32[]{:S(2)}, u32[]{:S(2)}) async-start(bf16[16,72,128]{2,1,0:T(8,128)(2,1)} %add_convert_fusion), calls=%async_computation | async-start | bytes 589824 | tf_op jit(solution)/shard_map/all_to_all | solution.py:422
  25.2 0.1 collective-permute-start.1
  25.2 6.4 %collective-permute-done.2.refs_2_ = bf16[16,16,1024]{2,1,0:T(8,128)(2,1)S(1)} collective-permute-done((bf16[16,16,1024]{2,1,0:T(8,128)(2,1)S(1)}, bf16[16,16,1024]{2,1,0:T(8,128)(2,1)S(1)}, u32[]{:S(2)}, u32[]{:S(2)}) %collective-permute-start.2) | collective-permute-done | bytes 524320 | tf_op jit(solution)/shard_map/ppermute | solution.py:412
  31.6 0.0 collective-permute-start.3
  31.6 4.5 %all-to-all-done.arrived = bf16[16,72,128]{2,1,0:T(8,128)(2,1)S(1)} async-done(((bf16[16,72,128]{2,1,0:T(8,128)(2,1)}), bf16[16,72,128]{2,1,0:T(8,128)(2,1)S(1)}, u32[]{:S(2)}, u32[]{:S(2)}) %all-to-all-start) | async-done | bytes 294944 | tf_op jit(solution)/shard_map/all_to_all | solution.py:422
  36.1 2.2 %transforms.1 = (f32[8,128]{1,0:T(8,128)S(1)}, bf16[64,128]{1,0:T(8,128)(2,1)S(1)}, bf16[64,128]{1,0:T(8,128)(2,1)S(1)}, bf16[64,128]{1,0:T(8,128)(2,1)S(1)}, bf16[64,128]{1,0:T(8,128)(2,1)S(1)}) custom-call(bf16[16,72,128]{2,1,0:T(8,128)(2,1)S(1)} %all-to-all-done.arrived), custom_call_target="tpu_custom_call" | custom-call | tf_op jit(solution)/shard_map/transforms/pallas_call | solution.py:287
  38.3 0.1 collective-permute-start.4
  38.4 0.6 %collective-permute-start.5 = (bf16[64,128]{1,0:T(8,128)(2,1)S(1)}, bf16[64,128]{1,0:T(8,128)(2,1)S(1)}, u32[]{:S(2)}, u32[]{:S(2)}) collective-permute-start(bf16[64,128]{1,0:T(8,128)(2,1)S(1)} %get-tuple-element.20), channel_id=1, source_target_pairs={{0,2},{1,3},{2,0},{3,1},{4,6},{5,7},{6,4},{7,5},{8,10},{9,11},{10,... | collective-permute-start | bytes 49160 | tf_op jit(solution)/shard_map/ppermute | solution.py:412
  39.0 1.2 %collective-permute-start.6 = (bf16[64,128]{1,0:T(8,128)(2,1)S(1)}, bf16[64,128]{1,0:T(8,128)(2,1)S(1)}, u32[]{:S(2)}, u32[]{:S(2)}) collective-permute-start(bf16[64,128]{1,0:T(8,128)(2,1)S(1)} %get-tuple-element.21), channel_id=1, source_target_pairs={{0,3},{1,2},{2,1},{3,0},{4,7},{5,6},{6,5},{7,4},{8,11},{9,10},{10,... | collective-permute-start | bytes 49160 | tf_op jit(solution)/shard_map/ppermute | solution.py:412
  40.3 0.9 %centre.1 = (bf16[1024,1024]{1,0:T(8,128)(2,1)S(1)}, f32[16,1024]{1,0:T(8,128)S(1)}) custom-call(bf16[16,16,1024]{2,1,0:T(8,128)(2,1)S(1)} %copy-done.1, bf16[16,16,1024]{2,1,0:T(8,128)(2,1)S(1)} %collective-permute-done.1.refs_1_, bf16[16,16,1024]{2,1,0:T(8,128)(2,1)S(1)} %collective-permute-done.2.refs_2_, ...), custom_call_target="tpu_custom_call" | custom-call | tf_op jit(solution)/shard_map/centre/pallas_call | solution.py:326
  41.2 1.2 %collective-permute-done.5.refs_2_ = bf16[64,128]{1,0:T(8,128)(2,1)S(1)} collective-permute-done((bf16[64,128]{1,0:T(8,128)(2,1)S(1)}, bf16[64,128]{1,0:T(8,128)(2,1)S(1)}, u32[]{:S(2)}, u32[]{:S(2)}) %collective-permute-start.5) | collective-permute-done | bytes 16416 | tf_op jit(solution)/shard_map/ppermute | solution.py:412
  42.4 2.3 %apply.1 = (bf16[256,1024]{1,0:T(8,128)(2,1)}, bf16[4,1024]{1,0:T(4,128)(2,1)}) custom-call(f32[8,128]{1,0:T(8,128)S(1)} %get-tuple-element.15.weights, bf16[1024,1024]{1,0:T(8,128)(2,1)S(1)} %get-tuple-element.16.pert, f32[16,1024]{1,0:T(8,128)S(1)} %get-tuple-element.17.mean, bf16[64,128]{1,0:T(8,128)(2,1)S(1)} %get-tuple-element.18.refs_0_, ...), custom_call_target="tpu_custom_call" | custom-call | tf_op jit(solution)/shard_map/apply/pallas_call | solution.py:386
  (13 shorter events, 0.0 us)
Async XLA Ops:
  0.6 1.6 %copy-start = (bf16[128,64,128]{2,1,0:T(8,128)(2,1)S(1)}, bf16[128,64,128]{2,1,0:T(8,128)(2,1)}, u32[]{:S(2)}) copy-start(bf16[128,64,128]{2,1,0:T(8,128)(2,1)} %refs_6_.1) | copy-start | bytes 6291460
  2.2 0.8 %copy-start.2 = (f32[128,128]{1,0:T(8,128)S(1)}, f32[128,128]{1,0:T(8,128)}, u32[]{:S(2)}) copy-start(f32[128,128]{1,0:T(8,128)} %refs_4_.1) | copy-start | bytes 196612
  3.1 0.8 %copy-start.3 = (f32[128,128]{1,0:T(8,128)S(1)}, f32[128,128]{1,0:T(8,128)}, u32[]{:S(2)}) copy-start(f32[128,128]{1,0:T(8,128)} %refs_5_.1) | copy-start | bytes 196612
  3.9 0.7 %copy-start.4 = (s32[128]{0:T(128)S(1)}, s32[128]{0:T(128)}, u32[]{:S(2)}) copy-start(s32[128]{0:T(128)} %refs_0_.2) | copy-start | bytes 1540
  4.6 0.7 %copy-start.5 = (s32[128]{0:T(128)S(1)}, s32[128]{0:T(128)}, u32[]{:S(2)}) copy-start(s32[128]{0:T(128)} %refs_1_.1) | copy-start | bytes 1540
  5.2 0.7 %copy-start.6 = (s32[128]{0:T(128)S(1)}, s32[128]{0:T(128)}, u32[]{:S(2)}) copy-start(s32[128]{0:T(128)} %refs_2_.1) | copy-start | bytes 1540
  5.9 0.7 %copy-start.7 = (s32[128]{0:T(128)S(1)}, s32[128]{0:T(128)}, u32[]{:S(2)}) copy-start(s32[128]{0:T(128)} %refs_3_.1) | copy-start | bytes 1540
  6.5 8.4 %copy-start.1 = (bf16[16,16,1024]{2,1,0:T(8,128)(2,1)S(1)}, bf16[16,16,1024]{2,1,0:T(8,128)(2,1)}, u32[]{:S(2)}) copy-start(bf16[16,16,1024]{2,1,0:T(8,128)(2,1)} %refs_0_.3) | copy-start | bytes 1572868
  14.4 3.2 %collective-permute-start = (bf16[16,72,128]{2,1,0:T(8,128)(2,1)S(1)}, bf16[16,72,128]{2,1,0:T(8,128)(2,1)S(1)}, u32[]{:S(2)}, u32[]{:S(2)}) collective-permute-start(bf16[16,72,128]{2,1,0:T(8,128)(2,1)S(1)} %get-tuple-element.14), channel_id=1, source_target_pairs={{0,1},{1,0},{2,3},{3,2},{4,5},{5,4},{6,7},{7,6},{8,9},{9,8},{10,11... | collective-permute-start | bytes 884744 | tf_op jit(solution)/shard_map/ppermute | solution.py:420
  14.9 16.7 %collective-permute-start.2 = (bf16[16,16,1024]{2,1,0:T(8,128)(2,1)S(1)}, bf16[16,16,1024]{2,1,0:T(8,128)(2,1)S(1)}, u32[]{:S(2)}, u32[]{:S(2)}) collective-permute-start(bf16[16,16,1024]{2,1,0:T(8,128)(2,1)S(1)} %copy-done.1), channel_id=1, source_target_pairs={{0,2},{1,3},{2,0},{3,1},{4,6},{5,7},{6,4},{7,5},{8,10},{9,11},{10,... | collective-permute-start | bytes 1572872 | tf_op jit(solution)/shard_map/ppermute | solution.py:412
  18.3 17.8 %all-to-all-start = ((bf16[16,72,128]{2,1,0:T(8,128)(2,1)}), bf16[16,72,128]{2,1,0:T(8,128)(2,1)S(1)}, u32[]{:S(2)}, u32[]{:S(2)}) async-start(bf16[16,72,128]{2,1,0:T(8,128)(2,1)} %add_convert_fusion), calls=%async_computation | async-start | bytes 589824 | tf_op jit(solution)/shard_map/all_to_all | solution.py:422
  25.2 15.1 %collective-permute-start.1 = (bf16[16,16,1024]{2,1,0:T(8,128)(2,1)S(1)}, bf16[16,16,1024]{2,1,0:T(8,128)(2,1)S(1)}, u32[]{:S(2)}, u32[]{:S(2)}) collective-permute-start(bf16[16,16,1024]{2,1,0:T(8,128)(2,1)S(1)} %copy-done.1), channel_id=1, source_target_pairs={{0,1},{1,0},{2,3},{3,2},{4,5},{5,4},{6,7},{7,6},{8,9},{9,8},{10,11... | collective-permute-start | bytes 1572872 | tf_op jit(solution)/shard_map/ppermute | solution.py:412
  31.6 8.6 %collective-permute-start.3 = (bf16[16,16,1024]{2,1,0:T(8,128)(2,1)S(1)}, bf16[16,16,1024]{2,1,0:T(8,128)(2,1)S(1)}, u32[]{:S(2)}, u32[]{:S(2)}) collective-permute-start(bf16[16,16,1024]{2,1,0:T(8,128)(2,1)S(1)} %collective-permute-done.2.refs_2_), channel_id=1, source_target_pairs={{0,1},{1,0},{2,3},{3,2},{4,5},{5,4},{6,7},{7,6},{8,9},{9,8},{10,11... | collective-permute-start | bytes 1572872 | tf_op jit(solution)/shard_map/ppermute | solution.py:425
  38.3 2.9 %collective-permute-start.4 = (bf16[64,128]{1,0:T(8,128)(2,1)S(1)}, bf16[64,128]{1,0:T(8,128)(2,1)S(1)}, u32[]{:S(2)}, u32[]{:S(2)}) collective-permute-start(bf16[64,128]{1,0:T(8,128)(2,1)S(1)} %get-tuple-element.19), channel_id=1, source_target_pairs={{0,1},{1,0},{2,3},{3,2},{4,5},{5,4},{6,7},{7,6},{8,9},{9,8},{10,11... | collective-permute-start | bytes 49160 | tf_op jit(solution)/shard_map/ppermute | solution.py:412
  38.4 4.0 %collective-permute-start.5 = (bf16[64,128]{1,0:T(8,128)(2,1)S(1)}, bf16[64,128]{1,0:T(8,128)(2,1)S(1)}, u32[]{:S(2)}, u32[]{:S(2)}) collective-permute-start(bf16[64,128]{1,0:T(8,128)(2,1)S(1)} %get-tuple-element.20), channel_id=1, source_target_pairs={{0,2},{1,3},{2,0},{3,1},{4,6},{5,7},{6,4},{7,5},{8,10},{9,11},{10,... | collective-permute-start | bytes 49160 | tf_op jit(solution)/shard_map/ppermute | solution.py:412
  39.0 3.3 %collective-permute-start.6 = (bf16[64,128]{1,0:T(8,128)(2,1)S(1)}, bf16[64,128]{1,0:T(8,128)(2,1)S(1)}, u32[]{:S(2)}, u32[]{:S(2)}) collective-permute-start(bf16[64,128]{1,0:T(8,128)(2,1)S(1)} %get-tuple-element.21), channel_id=1, source_target_pairs={{0,3},{1,2},{2,1},{3,0},{4,7},{5,6},{6,5},{7,4},{8,11},{9,10},{10,... | collective-permute-start | bytes 49160 | tf_op jit(solution)/shard_map/ppermute | solution.py:412

commit v3 on v2

--- a/solution.py
+++ b/solution.py
@@ -19,6 +19,10 @@
 
 def iota(shape, dim):
     return lax.broadcasted_iota(jnp.int32, shape, dim)
+
+
+def my_group():
+    return (lax.axis_index("yhi") * 2 + lax.axis_index("ylo")) * CORES + lax.axis_index("core")
 
 
 def packed_rows(own):
@@ -42,8 +46,8 @@
 
 
 def gram_kernel(own, chunks, *refs):
-    sources, (send, keep) = refs[:7], refs[7:9]
-    held, total, sems = refs[9:16], refs[16], refs[17]
+    sources, (send, total) = refs[:7], refs[7:9]
+    held, sems = refs[9:16], refs[16]
     count, tile, block, turn, values, weight, members = held
     blocks, size, rows = members.shape
     per_chunk = blocks // chunks
@@ -102,51 +106,129 @@
         def step(i, _):
             return add_pair(c * half_chunk + i)
 
-        return lax.fori_loop(0, half_chunk, step, 0, unroll=4)
+        return lax.fori_loop(0, half_chunk, step, 0, unroll=16)
 
     lax.fori_loop(0, chunks, add_chunk, 0)
 
+    pack_side(own, size, total, send, 1 - lax.axis_index("core"))
+
+
+def pack_side(own, size, total, out, side):
     half = size // 2
-    lane_half = iota((half, LANES), 1)
-    col = lane_half % size
+    col = iota((half, LANES), 1) % size
     row = iota((half, LANES), 0)
     from_top = (col >= half) | (col <= row)
     on_diag = col == row
-    core = lax.axis_index("core")
+    in_first = iota((size, LANES), 1) < size
     row8 = iota((8, LANES), 0)
 
     def halves_added(even, odd, mask):
         one = jnp.where(mask, even, odd)
         two = jnp.where(mask, odd, even)
-        return one, pltpu.roll(two, size, 1)
-
-    def pack(d, side):
+        return one + pltpu.roll(two, size, 1)
+
+    def pack(d, _):
         base = d * (CORES * own) + side * own
-        bodies = []
         tail = jnp.zeros((8, LANES), F32)
         for pair in range(own // 2):
             even, odd = base + 2 * pair, base + 2 * pair + 1
-            both = sum(halves_added(total[even, :size], total[odd, :size], in_first))
+            both = halves_added(total[even, :size], total[odd, :size], in_first)
             top = both[:half]
             bottom = pltpu.roll(both[half:size], LANES - half, 1)
-            bodies.append(jnp.where(from_top, top, bottom))
+            folded = jnp.where(from_top, top, bottom)
+            out[d, half * pair : half * (pair + 1)] = folded.astype(out.dtype)
             diag = jnp.sum(jnp.where(on_diag, bottom, 0.0), axis=0, keepdims=True)
-            one, two = halves_added(total[even, size:], total[odd, size:], in_first[:8])
-            projections = jnp.sum(one + two, axis=0, keepdims=True)
-            tail = jnp.where(row8 == 2 * pair, projections, tail)
+            ends = halves_added(total[even, size:], total[odd, size:], in_first[:8])
+            tail = jnp.where(row8 == 2 * pair, jnp.sum(ends, axis=0, keepdims=True), tail)
             tail = jnp.where(row8 == 2 * pair + 1, diag, tail)
-        return jnp.concatenate(bodies + [tail], axis=0)
-
-    def pack_both(d, _):
-        keep[d] = pack(d, core)
-        send[d] = pack(d, 1 - core).astype(BF16)
+        out[d, 16 * own :] = tail.astype(out.dtype)
         return 0
 
-    lax.fori_loop(0, send.shape[0], pack_both, 0)
+    lax.fori_loop(0, out.shape[0], pack, 0, unroll=2)
+
+
+def keep_kernel(own, size, total, keep):
+    pack_side(own, size, total, keep, lax.axis_index("core"))
+
+
+def kept(own, size, total):
+    dests = total.shape[0] // (CORES * own)
+    return pl.pallas_call(
+        functools.partial(keep_kernel, own, size),
+        out_shape=jax.ShapeDtypeStruct((dests, packed_rows(own), LANES), F32),
+        in_specs=[whole()],
+        out_specs=whole(),
+        compiler_params=params(total.size * 4 // (1024 * 1024) + 8),
+        name="keep",
+    )(total)
+
+
+def plane_kernel(highs, keep, got, mine, *outs):
+    rows_high = highs[1]
+    tlo, ylo = lax.axis_index("tlo"), lax.axis_index("ylo")
+
+    def one(slot, _):
+        for r in range(4):
+            tile = (slot // rows_high) * 2 + (tlo ^ (r // 2))
+            row = (slot % rows_high) * 2 + (ylo ^ (r % 2))
+            d = tile * (2 * rows_high) + row
+            both = keep[d] + got[d].astype(F32)
+            if r == 0:
+                mine[slot] = both
+            else:
+                outs[r - 1][slot] = both.astype(BF16)
+        return 0
+
+    lax.fori_loop(0, mine.shape[0], one, 0)
+
+
+def plane_parts(highs, keep, got):
+    slots = highs[0] * highs[1]
+    shape = (slots,) + keep.shape[1:]
+    return pl.pallas_call(
+        functools.partial(plane_kernel, highs),
+        out_shape=(jax.ShapeDtypeStruct(shape, F32),) + (jax.ShapeDtypeStruct(shape, BF16),) * 3,
+        in_specs=[whole()] * 2,
+        out_specs=(whole(),) * 4,
+        compiler_params=params(12),
+        name="plane",
+    )(keep, got)
+
+
+def line_kernel(stacked, *refs):
+    mine, got, outs = refs[0], refs[1:4], refs[4:]
+    z = lax.axis_index("thi") if not stacked else 0
+    for s in range(mine.shape[0]):
+        at = s if stacked else z ^ s
+        total = mine[at] + sum(g[at].astype(F32) for g in got)
+        if stacked:
+            outs[0][s] = total.astype(BF16)
+        else:
+            outs[s][...] = total.astype(outs[s].dtype)
+
+
+def line_parts(stacked, mine, got):
+    slots, one = mine.shape[0], mine.shape[1:]
+    if stacked:
+        shapes = (jax.ShapeDtypeStruct(mine.shape, BF16),)
+    else:
+        shapes = (jax.ShapeDtypeStruct(one, F32),) + (jax.ShapeDtypeStruct(one, BF16),) * (slots - 1)
+    return pl.pallas_call(
+        functools.partial(line_kernel, stacked),
+        out_shape=shapes,
+        in_specs=[whole()] * 4,
+        out_specs=(whole(),) * len(shapes),
+        compiler_params=params(12),
+        name="line",
+    )(mine, *got)
 
 
 def hbm():
     return pl.BlockSpec(memory_space=pltpu.HBM)
+
+
+def stay(x):
+    return pltpu.with_memory_space_constraint(x, pltpu.HBM)
 
 
 def params(mib):
@@ -158,22 +240,22 @@
     dests = tiles * ABLK // (CORES * own)
     shape = (dests, packed_rows(own), LANES)
     chunks = 4
-    small = tiles * ABLK * (size + 8) * LANES * 4 // (1024 * 1024)
+    sums = (tiles * ABLK, size + 8, LANES)
+    mib = tiles * ABLK * (size + 8) * LANES * 4 // (1024 * 1024)
     return pl.pallas_call(
         functools.partial(gram_kernel, own, chunks),
-        out_shape=(jax.ShapeDtypeStruct(shape, BF16), jax.ShapeDtypeStruct(shape, F32)),
+        out_shape=(jax.ShapeDtypeStruct(shape, BF16), jax.ShapeDtypeStruct(sums, F32)),
         in_specs=[hbm()] * 7,
         out_specs=(whole(), whole()),
         scratch_shapes=[pltpu.SMEM((blocks,), jnp.int32)] * 4
         + [pltpu.VMEM((blocks, rows), F32)] * 2
         + [
             pltpu.VMEM((blocks, size, rows), BF16),
-            pltpu.VMEM((tiles * ABLK, size + 8, LANES), F32),
             pltpu.SemaphoreType.DMA((6 + chunks,)),
         ],
-        compiler_params=params(small + 12),
+        compiler_params=params(mib + 12),
         name="grams",
-    )(count, tile, block, turn, values, weight, members)
+    )(*(stay(x) for x in (count, tile, block, turn, values, weight, members)))
 
 
 def split(x):
@@ -195,11 +277,12 @@
     return jnp.dot(left, right, preferred_element_type=F32)
 
 
-def transform_kernel(own, size, groups, arrived, weights_out, *rest):
-    outs, spread = rest[:groups], rest[groups]
-    summed = arrived[0].astype(F32)
-    for s in range(1, arrived.shape[0]):
-        summed = summed + arrived[s].astype(F32)
+def transform_kernel(own, size, groups, *refs):
+    outs, spread, weights_out = refs[-groups - 1 : -1], refs[-1], refs[-groups - 2]
+    pieces = []
+    for ref in refs[: -groups - 2]:
+        pieces += [ref[...]] if len(ref.shape) == 2 else [ref[i] for i in range(ref.shape[0])]
+    summed = sum(piece.astype(F32) for piece in pieces)
     half = size // 2
     col = iota((half, LANES), 1) % size
     row = iota((half, LANES), 0)
@@ -264,7 +347,7 @@
                 times(left_of(z, first_half), right_of(e)) for z, e in zip(inverses, middles)
             ]
     share = size // groups
-    me = lax.axis_index("y") * CORES + lax.axis_index("core")
+    me = my_group()
     rows8 = iota((8, LANES), 0)
     weights = jnp.zeros((8, LANES), F32)
     for q in range(own):
@@ -288,12 +371,12 @@
         functools.partial(transform_kernel, own, size, groups),
         out_shape=(jax.ShapeDtypeStruct((8, LANES), F32),)
         + tuple(jax.ShapeDtypeStruct((own * share, LANES), BF16) for _ in range(groups)),
-        in_specs=[whole()],
+        in_specs=[whole()] * len(arrived),
         out_specs=tuple([whole()] * (groups + 1)),
         scratch_shapes=[pltpu.VMEM((own, size, LANES), F32)],
         compiler_params=params(8),
         name="transforms",
-    )(arrived)
+    )(*arrived)
 
 
 def centre_kernel(*refs):
@@ -341,7 +424,7 @@
     size_by_block, width = pert.shape
     share = arrived[0].shape[0] // own
     rows = share * ABLK
-    me = lax.axis_index("y") * CORES + lax.axis_index("core")
+    me = my_group()
     received = jnp.concatenate([r[...] for r in arrived], axis=0)
     per_source = own * share
     count = groups * per_source
@@ -401,41 +484,56 @@
 
 
 def body(ensemble, obs_members, obs_values, obs_weight, obs_count, obs_tile, obs_block, obs_turn):
-    tiles = lax.axis_size("tile")
-    groups = lax.axis_size("y") * CORES
+    highs = (lax.axis_size("thi"), lax.axis_size("yhi"))
+    tiles, groups = highs[0] * 2, highs[1] * 2 * CORES
     own = ABLK // groups
     size = obs_members.shape[1]
     across = [(i, i ^ 1) for i in range(CORES)]
 
-    def swapped(x, b):
-        pairs = [(i, i ^ b) for i in range(groups)]
-        return lax.ppermute(x, ("y", "core"), pairs)
-
-    far = [swapped(ensemble, b) for b in range(2, groups, 2)]
-    near = swapped(ensemble, 1)
-    send, keep = scaled_grams(
+    def swapped(x, b, axes, count):
+        return lax.ppermute(x, axes, [(i, i ^ b) for i in range(count)])
+
+    mem = ("yhi", "ylo", "core")
+    far = [swapped(ensemble, b, mem, groups) for b in range(2, groups, 2)]
+    near = swapped(ensemble, 1, mem, groups)
+    send, total = scaled_grams(
         own, obs_count, obs_tile, obs_block, obs_turn, obs_values, obs_weight,
         obs_members, tiles,
     )
     got = lax.ppermute(send, "core", across)
-    mine = (keep + got.astype(F32)).astype(BF16)
-    arrived = lax.all_to_all(mine, ("tile", "y"), split_axis=0, concat_axis=0, tiled=True)
+    keep = kept(own, size, total)
+    mine, *sends = plane_parts(highs, keep, got)
+    got = []
+    for r, x in enumerate(sends):
+        got.append(swapped(x, r + 1, ("tlo", "ylo"), 4))
+    stacked = highs[1] > 1 or highs[0] > 4
+    arrived = list(line_parts(stacked, mine, got))
+    if stacked:
+        arrived = [
+            lax.all_to_all(arrived[0], ("thi", "yhi"), split_axis=0, concat_axis=0, tiled=True)
+        ]
+    else:
+        for s in range(1, highs[0]):
+            arrived[s] = swapped(arrived[s], s, ("thi",), highs[0])
     parts = [ensemble, near]
     for x in far:
         parts += [x, lax.ppermute(x, "core", across)]
     pert, mean = centred(parts)
     weights, *spreads = transforms(own, size, groups, arrived)
-    spreads = [spreads[0]] + [swapped(s, b) for b, s in enumerate(spreads) if b]
+    for b in range(1, groups):
+        spreads[b] = swapped(spreads[b], b, mem, groups)
     analysis_pert, analysis_mean = applied(own, weights, pert, mean, spreads)
     return analysis_pert.reshape(ensemble.shape), analysis_mean
 
 
 def solution(mesh):
     tiles, groups = mesh.shape["tile"], mesh.shape["mem"]
-    fine = Mesh(mesh.devices.reshape(tiles, groups // CORES, CORES), ("tile", "y", "core"))
-    everyone = ("tile", "y", "core")
+    shape = (tiles // 2, 2, groups // (2 * CORES), 2, CORES)
+    fine = Mesh(mesh.devices.reshape(shape), ("thi", "tlo", "yhi", "ylo", "core"))
+    tile, mem = ("thi", "tlo"), ("yhi", "ylo", "core")
+    everyone = tile + mem
     placed = (
-        P(("y", "core"), "tile", None),
+        P(mem, tile, None),
         P(everyone, None, None),
         P(everyone, None),
         P(everyone, None),
@@ -448,6 +546,6 @@
         body,
         mesh=fine,
         in_specs=placed,
-        out_specs=(P(("y", "core"), "tile", None), P(everyone, None)),
+        out_specs=(P(mem, tile, None), P(everyone, None)),
         check_vma=False,
     )

time: 45.1 us -> 49.6 us (1.100)
  waiting for transfers between devices: 12.1 us -> 23.6 us
  local copies, waits for them, and re-layouts: 5.88 us -> 0.01 us
  Pallas kernels: 13.3 us -> 11.6 us
  starting transfers between devices: 12 us -> 13.6 us
  other arithmetic: 0.78 us -> 0 us
    ppermute x5 -> x11, waiting for transfers between devices: 7.55 us -> 23.6 us  [swapped(): return lax.ppermute(x, axes, [(i, i ^ b) for i in range(count)])]
    ppermute x5 -> x11, starting transfers between devices: 4.58 us -> 13 us  [swapped(): return lax.ppermute(x, axes, [(i, i ^ b) for i in range(count)])]
    all_to_all x1 -> x0, starting transfers between devices: 6.83 us -> none  [body(): lax.all_to_all(mine, ('tile', 'y'), split_axis=0, concat_axis=0, tiled=True)]
    unnamed x16 -> x2, local copies, waits for them, and re-layouts: 5.88 us -> 0.01 us
    all_to_all x1 -> x0, waiting for transfers between devices: 4.52 us -> none  [body(): lax.all_to_all(mine, ('tile', 'y'), split_axis=0, concat_axis=0, tiled=True)]
    pallas_call x1, Pallas kernels: 7.84 us -> 4.65 us  [scaled_grams(): pl.pallas_call(functools.partial(gram_kernel, own, chunks), out_shape=(ja...]
    pallas_call x0 -> x3, Pallas kernels: none -> 1.46 us  [the longest x1 1.32 us: kept(): pl.pallas_call(functools.partial(keep_kernel, own, size), out_shape=jax.S...]
    convert_element_type x1 -> x0, other arithmetic: 0.78 us -> none  [body(): mine = (keep + got.astype(F32)).astype(BF16)]
  transfers between devices with their start and end apart: 8 -> 13, of which waited for: 3 -> 8; matrix products, arithmetic and copies ran while one was open for 2% -> 0% of each run, Pallas kernels for 7% -> 19%
where the time goes in v3:
time: 49.6 us; the launch traced here: 49.5 us
  waiting for transfers between devices  23.6 us (48%)
  starting transfers between devices  13.6 us (27%)
  Pallas kernels  11.6 us (23%)
  between operations  0.71 us (1%)
    ppermute x11, waiting for transfers between devices, swapped(): return lax.ppermute(x, axes, [(i, i ^ b) for i in range(count)])  23.6 us
    ppermute x11, starting transfers between devices, swapped(): return lax.ppermute(x, axes, [(i, i ^ b) for i in range(count)])  13 us
    pallas_call x1, Pallas kernels, scaled_grams(): pl.pallas_call(functools.partial(gram_kernel, own, chunks), out_shape=(ja...  4.65 us
    pallas_call x1, Pallas kernels, applied(): pl.pallas_call(functools.partial(apply_kernel, own, groups), out_shape=(j...  2.34 us
    pallas_call x1, Pallas kernels, transforms(): pl.pallas_call(functools.partial(transform_kernel, own, size, groups), ou...  2.17 us
    pallas_call x1, Pallas kernels, kept(): pl.pallas_call(functools.partial(keep_kernel, own, size), out_shape=jax.S...  1.32 us
  transfers between devices with their start and end apart: 13, of which 8 were waited for; matrix products, arithmetic and copies ran while one was open for 0% of the time, Pallas kernels for 19%

profile of v3, /device:TPU:0, one launch (start us, length us, event | category | flops | bytes accessed | tf_op | source)
XLA Modules:
  0.0 49.5 jit_solution(9996638895539128640)
XLA Ops:
  0.6 3.1 %collective-permute-start.8 = (bf16[16,16,1024]{2,1,0:T(8,128)(2,1)}, bf16[16,16,1024]{2,1,0:T(8,128)(2,1)S(1)}, u32[]{:S(2)}, u32[]{:S(2)}) collective-permute-start(bf16[16,16,1024]{2,1,0:T(8,128)(2,1)} %refs_0_.3), channel_id=1, source_target_pairs={{0,2},{1,3},{2,0},{3,1},{4,6},{5,7},{6,4},{7,5},{8,10},{9,11},{10,... | collective-permute-start | bytes 1572872 | tf_op jit(solution)/shard_map/ppermute | solution.py:494
  3.7 12.1 %collective-permute-done.8.refs_2_ = bf16[16,16,1024]{2,1,0:T(8,128)(2,1)S(1)} collective-permute-done((bf16[16,16,1024]{2,1,0:T(8,128)(2,1)}, bf16[16,16,1024]{2,1,0:T(8,128)(2,1)S(1)}, u32[]{:S(2)}, u32[]{:S(2)}) %collective-permute-start.8) | collective-permute-done | bytes 524320 | tf_op jit(solution)/shard_map/ppermute | solution.py:494
  15.8 4.7 %grams.1 = (bf16[16,72,128]{2,1,0:T(8,128)(2,1)S(1)}, f32[128,72,128]{2,1,0:T(8,128)S(1)}) custom-call(s32[128]{0:T(128)} %refs_0_.2, s32[128]{0:T(128)} %refs_1_.1, s32[128]{0:T(128)} %refs_2_.1, s32[128]{0:T(128)} %refs_3_.1, f32[128,128]{1,0:T(8,128)} %refs_4_.1, f32[128,128]{1,0:T(8,128)} %refs_5_.1, bf16[128,64,128]{2,1,0:T(8,128)(2,1)} %refs_6_.1), custom_call_target="tpu_custom_call" | custom-call | tf_op jit(solution)/shard_map/grams/pallas_call | solution.py:245
  20.5 0.6 %collective-permute-start = (bf16[16,72,128]{2,1,0:T(8,128)(2,1)S(1)}, bf16[16,72,128]{2,1,0:T(8,128)(2,1)S(1)}, u32[]{:S(2)}, u32[]{:S(2)}) collective-permute-start(bf16[16,72,128]{2,1,0:T(8,128)(2,1)S(1)} %get-tuple-element.22), channel_id=1, source_target_pairs={{0,1},{1,0},{2,3},{3,2},{4,5},{5,4},{6,7},{7,6},{8,9},{9,8},{10,11... | collective-permute-start | bytes 884744 | tf_op jit(solution)/shard_map/ppermute | solution.py:503
  21.1 1.3 %keep.1 = f32[16,72,128]{2,1,0:T(8,128)S(1)} custom-call(f32[128,72,128]{2,1,0:T(8,128)S(1)} %get-tuple-element.21.total), custom_call_target="tpu_custom_call" | custom-call | tf_op jit(solution)/shard_map/keep/pallas_call | solution.py:156
  22.4 0.1 plane.1
  22.5 1.8 %collective-permute-start.1 = (bf16[4,72,128]{2,1,0:T(8,128)(2,1)S(1)}, bf16[4,72,128]{2,1,0:T(8,128)(2,1)S(1)}, u32[]{:S(2)}, u32[]{:S(2)}) collective-permute-start(bf16[4,72,128]{2,1,0:T(8,128)(2,1)S(1)} %get-tuple-element.24), channel_id=1, source_target_pairs={{0,2},{2,0},{4,6},{6,4},{1,3},{3,1},{5,7},{7,5},{8,10},{10,8},{12,... | collective-permute-start | bytes 221192 | tf_op jit(solution)/shard_map/ppermute | solution.py:494
  24.3 1.5 %collective-permute-start.2 = (bf16[4,72,128]{2,1,0:T(8,128)(2,1)S(1)}, bf16[4,72,128]{2,1,0:T(8,128)(2,1)S(1)}, u32[]{:S(2)}, u32[]{:S(2)}) collective-permute-start(bf16[4,72,128]{2,1,0:T(8,128)(2,1)S(1)} %get-tuple-element.25), channel_id=1, source_target_pairs={{0,4},{2,6},{4,0},{6,2},{1,5},{3,7},{5,1},{7,3},{8,12},{10,14},{12... | collective-permute-start | bytes 221192 | tf_op jit(solution)/shard_map/ppermute | solution.py:494
  25.8 0.2 collective-permute-start.3
  26.1 0.9 %collective-permute-done.1.refs_1_ = bf16[4,72,128]{2,1,0:T(8,128)(2,1)S(1)} collective-permute-done((bf16[4,72,128]{2,1,0:T(8,128)(2,1)S(1)}, bf16[4,72,128]{2,1,0:T(8,128)(2,1)S(1)}, u32[]{:S(2)}, u32[]{:S(2)}) %collective-permute-start.1) | collective-permute-done | bytes 73760 | tf_op jit(solution)/shard_map/ppermute | solution.py:494
  27.0 2.4 %collective-permute-done.2.refs_2_ = bf16[4,72,128]{2,1,0:T(8,128)(2,1)S(1)} collective-permute-done((bf16[4,72,128]{2,1,0:T(8,128)(2,1)S(1)}, bf16[4,72,128]{2,1,0:T(8,128)(2,1)S(1)}, u32[]{:S(2)}, u32[]{:S(2)}) %collective-permute-start.2) | collective-permute-done | bytes 73760 | tf_op jit(solution)/shard_map/ppermute | solution.py:494
  29.3 1.7 %collective-permute-done.3.refs_3_ = bf16[4,72,128]{2,1,0:T(8,128)(2,1)S(1)} collective-permute-done((bf16[4,72,128]{2,1,0:T(8,128)(2,1)S(1)}, bf16[4,72,128]{2,1,0:T(8,128)(2,1)S(1)}, u32[]{:S(2)}, u32[]{:S(2)}) %collective-permute-start.3) | collective-permute-done | bytes 73760 | tf_op jit(solution)/shard_map/ppermute | solution.py:494
  31.1 1.6 %collective-permute-start.4 = (bf16[72,128]{1,0:T(8,128)(2,1)S(1)}, bf16[72,128]{1,0:T(8,128)(2,1)S(1)}, u32[]{:S(2)}, u32[]{:S(2)}) collective-permute-start(bf16[72,128]{1,0:T(8,128)(2,1)S(1)} %get-tuple-element.28), channel_id=1, source_target_pairs={{0,8},{8,0},{16,24},{24,16},{1,9},{9,1},{17,25},{25,17},{2,10},{10... | collective-permute-start | bytes 55304 | tf_op jit(solution)/shard_map/ppermute | solution.py:494
  32.7 2.6 %collective-permute-start.5 = (bf16[72,128]{1,0:T(8,128)(2,1)S(1)}, bf16[72,128]{1,0:T(8,128)(2,1)S(1)}, u32[]{:S(2)}, u32[]{:S(2)}) collective-permute-start(bf16[72,128]{1,0:T(8,128)(2,1)S(1)} %get-tuple-element.29), channel_id=1, source_target_pairs={{0,16},{8,24},{16,0},{24,8},{1,17},{9,25},{17,1},{25,9},{2,18},{10... | collective-permute-start | bytes 55304 | tf_op jit(solution)/shard_map/ppermute | solution.py:494
  35.3 0.2 collective-permute-start.6
  35.6 1.9 %collective-permute-done.5.refs_2_ = bf16[72,128]{1,0:T(8,128)(2,1)S(1)} collective-permute-done((bf16[72,128]{1,0:T(8,128)(2,1)S(1)}, bf16[72,128]{1,0:T(8,128)(2,1)S(1)}, u32[]{:S(2)}, u32[]{:S(2)}) %collective-permute-start.5) | collective-permute-done | bytes 18464 | tf_op jit(solution)/shard_map/ppermute | solution.py:494
  37.5 3.4 %collective-permute-done.6.refs_3_ = bf16[72,128]{1,0:T(8,128)(2,1)S(1)} collective-permute-done((bf16[72,128]{1,0:T(8,128)(2,1)S(1)}, bf16[72,128]{1,0:T(8,128)(2,1)S(1)}, u32[]{:S(2)}, u32[]{:S(2)}) %collective-permute-start.6) | collective-permute-done | bytes 18464 | tf_op jit(solution)/shard_map/ppermute | solution.py:494
  40.9 2.2 %transforms.1 = (f32[8,128]{1,0:T(8,128)S(1)}, bf16[64,128]{1,0:T(8,128)(2,1)S(1)}, bf16[64,128]{1,0:T(8,128)(2,1)S(1)}, bf16[64,128]{1,0:T(8,128)(2,1)S(1)}, bf16[64,128]{1,0:T(8,128)(2,1)S(1)}) custom-call(f32[72,128]{1,0:T(8,128)S(1)} %get-tuple-element.27.refs_0_, bf16[72,128]{1,0:T(8,128)(2,1)S(1)} %collective-permute-done.4.refs_1_, ...), custom_call_target="tpu_custom_call" | custom-call | tf_op jit(solution)/shard_map/transforms/pallas_call | solution.py:370
  43.1 0.7 %collective-permute-start.11 = (bf16[64,128]{1,0:T(8,128)(2,1)S(1)}, bf16[64,128]{1,0:T(8,128)(2,1)S(1)}, u32[]{:S(2)}, u32[]{:S(2)}) collective-permute-start(bf16[64,128]{1,0:T(8,128)(2,1)S(1)} %get-tuple-element.36), channel_id=1, source_target_pairs={{0,2},{1,3},{2,0},{3,1},{4,6},{5,7},{6,4},{7,5},{8,10},{9,11},{10,... | collective-permute-start | bytes 49160 | tf_op jit(solution)/shard_map/ppermute | solution.py:494
  43.9 1.1 %collective-permute-start.12 = (bf16[64,128]{1,0:T(8,128)(2,1)S(1)}, bf16[64,128]{1,0:T(8,128)(2,1)S(1)}, u32[]{:S(2)}, u32[]{:S(2)}) collective-permute-start(bf16[64,128]{1,0:T(8,128)(2,1)S(1)} %get-tuple-element.37), channel_id=1, source_target_pairs={{0,3},{1,2},{2,1},{3,0},{4,7},{5,6},{6,5},{7,4},{8,11},{9,10},{10,... | collective-permute-start | bytes 49160 | tf_op jit(solution)/shard_map/ppermute | solution.py:494
  45.0 0.9 %centre.1 = (bf16[1024,1024]{1,0:T(8,128)(2,1)S(1)}, f32[16,1024]{1,0:T(8,128)S(1)}) custom-call(bf16[16,16,1024]{2,1,0:T(8,128)(2,1)S(1)} %copy-done, bf16[16,16,1024]{2,1,0:T(8,128)(2,1)S(1)} %collective-permute-done.7.refs_1_, bf16[16,16,1024]{2,1,0:T(8,128)(2,1)S(1)} %collective-permute-done.8.refs_2_, ...), custom_call_target="tpu_custom_call" | custom-call | tf_op jit(solution)/shard_map/centre/pallas_call | solution.py:409
  45.9 1.1 %collective-permute-done.11.refs_2_ = bf16[64,128]{1,0:T(8,128)(2,1)S(1)} collective-permute-done((bf16[64,128]{1,0:T(8,128)(2,1)S(1)}, bf16[64,128]{1,0:T(8,128)(2,1)S(1)}, u32[]{:S(2)}, u32[]{:S(2)}) %collective-permute-start.11) | collective-permute-done | bytes 16416 | tf_op jit(solution)/shard_map/ppermute | solution.py:494
  47.0 0.1 collective-permute-done.12.refs_3_
  47.1 2.3 %apply.1 = (bf16[256,1024]{1,0:T(8,128)(2,1)}, bf16[4,1024]{1,0:T(4,128)(2,1)}) custom-call(f32[8,128]{1,0:T(8,128)S(1)} %get-tuple-element.31.weights, bf16[1024,1024]{1,0:T(8,128)(2,1)S(1)} %get-tuple-element.32.pert, f32[16,1024]{1,0:T(8,128)S(1)} %get-tuple-element.33.mean, bf16[64,128]{1,0:T(8,128)(2,1)S(1)} %get-tuple-element.34.refs_0_, ...), custom_call_target="tpu_custom_call" | custom-call | tf_op jit(solution)/shard_map/apply/pallas_call | solution.py:469
  (11 shorter events, 0.1 us)
Async XLA Ops:
  0.6 15.2 %collective-permute-start.8 = (bf16[16,16,1024]{2,1,0:T(8,128)(2,1)}, bf16[16,16,1024]{2,1,0:T(8,128)(2,1)S(1)}, u32[]{:S(2)}, u32[]{:S(2)}) collective-permute-start(bf16[16,16,1024]{2,1,0:T(8,128)(2,1)} %refs_0_.3), channel_id=1, source_target_pairs={{0,2},{1,3},{2,0},{3,1},{4,6},{5,7},{6,4},{7,5},{8,10},{9,11},{10,... | collective-permute-start | bytes 1572872 | tf_op jit(solution)/shard_map/ppermute | solution.py:494
  3.7 41.3 %collective-permute-start.7 = (bf16[16,16,1024]{2,1,0:T(8,128)(2,1)}, bf16[16,16,1024]{2,1,0:T(8,128)(2,1)S(1)}, u32[]{:S(2)}, u32[]{:S(2)}) collective-permute-start(bf16[16,16,1024]{2,1,0:T(8,128)(2,1)} %refs_0_.3), channel_id=1, source_target_pairs={{0,1},{1,0},{2,3},{3,2},{4,5},{5,4},{6,7},{7,6},{8,9},{9,8},{10,11... | collective-permute-start | bytes 1572872 | tf_op jit(solution)/shard_map/ppermute | solution.py:494
  15.8 29.2 %collective-permute-start.9 = (bf16[16,16,1024]{2,1,0:T(8,128)(2,1)S(1)}, bf16[16,16,1024]{2,1,0:T(8,128)(2,1)S(1)}, u32[]{:S(2)}, u32[]{:S(2)}) collective-permute-start(bf16[16,16,1024]{2,1,0:T(8,128)(2,1)S(1)} %collective-permute-done.8.refs_2_), channel_id=1, source_target_pairs={{0,1},{1,0},{2,3},{3,2},{4,5},{5,4},{6,7},{7,6},{8,9},{9,8},{10,11... | collective-permute-start | bytes 1572872 | tf_op jit(solution)/shard_map/ppermute | solution.py:520
  20.5 1.9 %collective-permute-start = (bf16[16,72,128]{2,1,0:T(8,128)(2,1)S(1)}, bf16[16,72,128]{2,1,0:T(8,128)(2,1)S(1)}, u32[]{:S(2)}, u32[]{:S(2)}) collective-permute-start(bf16[16,72,128]{2,1,0:T(8,128)(2,1)S(1)} %get-tuple-element.22), channel_id=1, source_target_pairs={{0,1},{1,0},{2,3},{3,2},{4,5},{5,4},{6,7},{7,6},{8,9},{9,8},{10,11... | collective-permute-start | bytes 884744 | tf_op jit(solution)/shard_map/ppermute | solution.py:503
  21.1 23.9 %copy-start = (bf16[16,16,1024]{2,1,0:T(8,128)(2,1)S(1)}, bf16[16,16,1024]{2,1,0:T(8,128)(2,1)}, u32[]{:S(2)}) copy-start(bf16[16,16,1024]{2,1,0:T(8,128)(2,1)} %refs_0_.3) | copy-start | bytes 1572868
  22.5 4.5 %collective-permute-start.1 = (bf16[4,72,128]{2,1,0:T(8,128)(2,1)S(1)}, bf16[4,72,128]{2,1,0:T(8,128)(2,1)S(1)}, u32[]{:S(2)}, u32[]{:S(2)}) collective-permute-start(bf16[4,72,128]{2,1,0:T(8,128)(2,1)S(1)} %get-tuple-element.24), channel_id=1, source_target_pairs={{0,2},{2,0},{4,6},{6,4},{1,3},{3,1},{5,7},{7,5},{8,10},{10,8},{12,... | collective-permute-start | bytes 221192 | tf_op jit(solution)/shard_map/ppermute | solution.py:494
  24.3 5.0 %collective-permute-start.2 = (bf16[4,72,128]{2,1,0:T(8,128)(2,1)S(1)}, bf16[4,72,128]{2,1,0:T(8,128)(2,1)S(1)}, u32[]{:S(2)}, u32[]{:S(2)}) collective-permute-start(bf16[4,72,128]{2,1,0:T(8,128)(2,1)S(1)} %get-tuple-element.25), channel_id=1, source_target_pairs={{0,4},{2,6},{4,0},{6,2},{1,5},{3,7},{5,1},{7,3},{8,12},{10,14},{12... | collective-permute-start | bytes 221192 | tf_op jit(solution)/shard_map/ppermute | solution.py:494
  25.8 5.3 %collective-permute-start.3 = (bf16[4,72,128]{2,1,0:T(8,128)(2,1)S(1)}, bf16[4,72,128]{2,1,0:T(8,128)(2,1)S(1)}, u32[]{:S(2)}, u32[]{:S(2)}) collective-permute-start(bf16[4,72,128]{2,1,0:T(8,128)(2,1)S(1)} %get-tuple-element.26), channel_id=1, source_target_pairs={{0,6},{2,4},{4,2},{6,0},{1,7},{3,5},{5,3},{7,1},{8,14},{10,12},{12... | collective-permute-start | bytes 221192 | tf_op jit(solution)/shard_map/ppermute | solution.py:494
  31.1 4.5 %collective-permute-start.4 = (bf16[72,128]{1,0:T(8,128)(2,1)S(1)}, bf16[72,128]{1,0:T(8,128)(2,1)S(1)}, u32[]{:S(2)}, u32[]{:S(2)}) collective-permute-start(bf16[72,128]{1,0:T(8,128)(2,1)S(1)} %get-tuple-element.28), channel_id=1, source_target_pairs={{0,8},{8,0},{16,24},{24,16},{1,9},{9,1},{17,25},{25,17},{2,10},{10... | collective-permute-start | bytes 55304 | tf_op jit(solution)/shard_map/ppermute | solution.py:494
  32.7 4.7 %collective-permute-start.5 = (bf16[72,128]{1,0:T(8,128)(2,1)S(1)}, bf16[72,128]{1,0:T(8,128)(2,1)S(1)}, u32[]{:S(2)}, u32[]{:S(2)}) collective-permute-start(bf16[72,128]{1,0:T(8,128)(2,1)S(1)} %get-tuple-element.29), channel_id=1, source_target_pairs={{0,16},{8,24},{16,0},{24,8},{1,17},{9,25},{17,1},{25,9},{2,18},{10... | collective-permute-start | bytes 55304 | tf_op jit(solution)/shard_map/ppermute | solution.py:494
  35.3 5.6 %collective-permute-start.6 = (bf16[72,128]{1,0:T(8,128)(2,1)S(1)}, bf16[72,128]{1,0:T(8,128)(2,1)S(1)}, u32[]{:S(2)}, u32[]{:S(2)}) collective-permute-start(bf16[72,128]{1,0:T(8,128)(2,1)S(1)} %get-tuple-element.30), channel_id=1, source_target_pairs={{0,24},{8,16},{16,8},{24,0},{1,25},{9,17},{17,9},{25,1},{2,26},{10... | collective-permute-start | bytes 55304 | tf_op jit(solution)/shard_map/ppermute | solution.py:494
  43.1 2.9 %collective-permute-start.10 = (bf16[64,128]{1,0:T(8,128)(2,1)S(1)}, bf16[64,128]{1,0:T(8,128)(2,1)S(1)}, u32[]{:S(2)}, u32[]{:S(2)}) collective-permute-start(bf16[64,128]{1,0:T(8,128)(2,1)S(1)} %get-tuple-element.35), channel_id=1, source_target_pairs={{0,1},{1,0},{2,3},{3,2},{4,5},{5,4},{6,7},{7,6},{8,9},{9,8},{10,11... | collective-permute-start | bytes 49160 | tf_op jit(solution)/shard_map/ppermute | solution.py:494
  43.1 3.9 %collective-permute-start.11 = (bf16[64,128]{1,0:T(8,128)(2,1)S(1)}, bf16[64,128]{1,0:T(8,128)(2,1)S(1)}, u32[]{:S(2)}, u32[]{:S(2)}) collective-permute-start(bf16[64,128]{1,0:T(8,128)(2,1)S(1)} %get-tuple-element.36), channel_id=1, source_target_pairs={{0,2},{1,3},{2,0},{3,1},{4,6},{5,7},{6,4},{7,5},{8,10},{9,11},{10,... | collective-permute-start | bytes 49160 | tf_op jit(solution)/shard_map/ppermute | solution.py:494
  43.9 3.3 %collective-permute-start.12 = (bf16[64,128]{1,0:T(8,128)(2,1)S(1)}, bf16[64,128]{1,0:T(8,128)(2,1)S(1)}, u32[]{:S(2)}, u32[]{:S(2)}) collective-permute-start(bf16[64,128]{1,0:T(8,128)(2,1)S(1)} %get-tuple-element.37), channel_id=1, source_target_pairs={{0,3},{1,2},{2,1},{3,0},{4,7},{5,6},{6,5},{7,4},{8,11},{9,10},{10,... | collective-permute-start | bytes 49160 | tf_op jit(solution)/shard_map/ppermute | solution.py:494
